TPU v7x, 32 devices: a whole 2x2x4 slice. The times are simulated.
32 devices in a mesh: dp: 2 (over x), ep: 16 (over z, y, core).
Axes of the slice: x: 2, y: 2, z: 4, core: 2. Of those that a mesh axis runs over, the one named last changes fastest.
Arguments:
- grad_y: bfloat16 [8192, 1024], P(('dp', 'ep')), parts along dimension 0
- gate_vals: float32 [8192, 8], P(('dp', 'ep')), parts along dimension 0
- topk_idx: int32 [8192, 8], P(('dp', 'ep')), parts along dimension 0
- slot_ids: int32 [8192, 8], P(('dp', 'ep')), parts along dimension 0
- pair_counts: int32 [32, 32], P(('dp', 'ep')), parts along dimension 0
- y_routed: bfloat16 [8192, 8, 1024], P(('dp', 'ep')), parts along dimension 0
- x_disp: bfloat16 [64, 2048, 1024], P(('dp', 'ep')), parts along dimension 0
- h_gate: bfloat16 [64, 2048, 512], P(('dp', 'ep')), parts along dimension 0
- h_up: bfloat16 [64, 2048, 512], P(('dp', 'ep')), parts along dimension 0
- w_gate: bfloat16 [32, 1024, 512], P('ep')
- w_up: bfloat16 [32, 1024, 512], P('ep')
- w_down: bfloat16 [32, 512, 1024], P('ep')
Outputs:
- output 1: bfloat16 [8192, 1024], P(('dp', 'ep')), parts along dimension 0
- output 2: float32 [8192, 8], P(('dp', 'ep')), parts along dimension 0
- output 3: float32 [64, 1024, 512], P(('dp', 'ep')), parts along dimension 0
- output 4: float32 [64, 1024, 512], P(('dp', 'ep')), parts along dimension 0
- output 5: float32 [64, 512, 1024], P(('dp', 'ep')), parts along dimension 0
There are 2 independent parts. A program takes and returns all parts, laid end to end along the dimension named above; an argument that names none is the same for every part.
All inputs are finite; a program needn't handle non-finite values.
Results may differ from a plain program's by a relative error of at most 0.0149559.
Values are sent between devices in bfloat16 or wider.
A program may use at most 1 GiB of HBM per device.

v0:
```python
import jax
import jax.numpy as jnp
from jax import lax
from jax.sharding import PartitionSpec as P


def build_send(grad_y, gate_vals, topk_idx, slot_ids, n_exp, cap_rows):
    tok_dev, top_k = topk_idx.shape
    dest_row = jnp.where(slot_ids >= 0, topk_idx * cap_rows + slot_ids, n_exp * cap_rows).reshape(-1)
    row_source = jnp.full((n_exp * cap_rows,), tok_dev * top_k, jnp.int32).at[dest_row].set(jnp.arange(tok_dev * top_k, dtype=jnp.int32), mode="drop")
    dy_rows = jnp.take(grad_y, row_source // top_k, axis=0, mode="fill", fill_value=0)
    gate_rows = jnp.take(gate_vals.reshape(-1), row_source, mode="fill", fill_value=0)
    return (gate_rows[:, None] * dy_rows).astype(jnp.bfloat16).reshape(n_exp, cap_rows, grad_y.shape[1])


def gather_back(ret_rows, topk_idx, slot_ids, cap_rows):
    tok_dev, top_k = topk_idx.shape
    src_row = jnp.where(slot_ids >= 0, topk_idx * cap_rows + slot_ids, ret_rows.shape[0]).reshape(-1)
    picked = jnp.take(ret_rows, src_row, axis=0, mode="fill", fill_value=0).reshape(tok_dev, top_k, ret_rows.shape[1])
    return jnp.sum(picked, axis=1, dtype=jnp.float32).astype(jnp.bfloat16)


def expert_grads(grad_rows, x_rows, hg_rows, hu_rows, w_gate, w_up, w_down):
    grad_hidden = jnp.einsum("erd,efd->erf", grad_rows, w_down, preferred_element_type=jnp.float32).astype(jnp.bfloat16)
    gate_f = hg_rows.astype(jnp.float32)
    up_f = hu_rows.astype(jnp.float32)
    gate_sig = jax.nn.sigmoid(gate_f)
    gate_act = gate_f * gate_sig
    hidden_act = (gate_act * up_f).astype(jnp.bfloat16)
    grad_h = grad_hidden.astype(jnp.float32)
    grad_hgate = (grad_h * up_f * gate_sig * (1.0 + gate_f * (1.0 - gate_sig))).astype(jnp.bfloat16)
    grad_hup = (grad_h * gate_act).astype(jnp.bfloat16)
    grad_wdown = jnp.einsum("erf,erd->efd", hidden_act, grad_rows, preferred_element_type=jnp.float32)
    grad_wgate = jnp.einsum("erd,erf->edf", x_rows, grad_hgate, preferred_element_type=jnp.float32)
    grad_wup = jnp.einsum("erd,erf->edf", x_rows, grad_hup, preferred_element_type=jnp.float32)
    grad_disp = (jnp.einsum("erf,edf->erd", grad_hgate, w_gate, preferred_element_type=jnp.float32) + jnp.einsum("erf,edf->erd", grad_hup, w_up, preferred_element_type=jnp.float32)).astype(jnp.bfloat16)
    return grad_disp, grad_wgate, grad_wup, grad_wdown


def solution(mesh):
    n_dev = mesh.shape["ep"]
    rows_spec = P(("dp", "ep"), None)
    cube_spec = P(("dp", "ep"), None, None)
    weight_spec = P("ep", None, None)

    def local_step(grad_y, gate_vals, topk_idx, slot_ids, pair_counts, y_routed, x_disp, h_gate, h_up, w_gate, w_up, w_down):
        n_loc = w_gate.shape[0]
        n_exp = n_loc * n_dev
        cap_rows = x_disp.shape[1] // n_dev
        model_dim = grad_y.shape[1]
        grad_gate = jnp.einsum("td,tkd->tk", grad_y, y_routed, preferred_element_type=jnp.float32)
        send_rows = build_send(grad_y, gate_vals, topk_idx, slot_ids, n_exp, cap_rows)
        recv_rows = lax.all_to_all(send_rows.reshape(n_dev, n_loc, cap_rows, model_dim), "ep", 0, 1)
        recv_counts = lax.all_to_all(pair_counts.reshape(n_dev, n_loc), "ep", 0, 1)
        keep_row = lax.broadcasted_iota(jnp.int32, (n_loc, n_dev, cap_rows), 2) < recv_counts[:, :, None]
        grad_rows = jnp.where(keep_row[..., None], recv_rows, jnp.zeros((), jnp.bfloat16)).reshape(n_loc, n_dev * cap_rows, model_dim)
        grad_disp, grad_wgate, grad_wup, grad_wdown = expert_grads(grad_rows, x_disp, h_gate, h_up, w_gate, w_up, w_down)
        ret_rows = lax.all_to_all(grad_disp.reshape(n_loc, n_dev, cap_rows, model_dim), "ep", 1, 0)
        grad_x = gather_back(ret_rows.reshape(n_exp * cap_rows, model_dim), topk_idx, slot_ids, cap_rows)
        return grad_x, grad_gate, grad_wgate, grad_wup, grad_wdown

    return jax.shard_map(local_step, mesh=mesh, in_specs=(rows_spec, rows_spec, rows_spec, rows_spec, rows_spec, cube_spec, cube_spec, cube_spec, cube_spec, weight_spec, weight_spec, weight_spec), out_specs=(rows_spec, rows_spec, cube_spec, cube_spec, cube_spec), check_vma=False)
```

profile of v0, /device:TPU:19, one launch (start us, length us, event | category | flops | bytes accessed | tf_op | source)
XLA Modules:
  0.0 515.6 jit_solution(2643356779179765875)
XLA Ops:
  1.2 1.4 reduce.4
  3.3 6.5 %all-to-all-start = ((s32[16,2,1]{1,2,0:T(1,128)}), s32[16,2,1]{1,2,0:T(1,128)S(1)}, u32[]{:S(2)}, u32[]{:S(2)}) async-start(s32[16,2,1]{1,2,0:T(1,128)} %bitcast.1), calls=%async_computation | async-start | bytes 16384 | tf_op jit(solution)/shard_map/all_to_all | solution.py:54
  10.8 8.1 %scatter_custom_fusion = s32[4096]{0:T(1024)S(1)} fusion(s32[2048]{0:T(1024)S(1)} %bitcast.52, s32[2048]{0:T(1024)S(1)} %iota.18, s32[]{:T(128)} %constant.61.clone.1), kind=kCustom, calls=%fused_computation.49 | custom fusion | bytes 16388 | tf_op jit(solution)/shard_map/scatter | solution.py:10
  18.9 0.8 copy.53
  19.8 23.0 %gather_fusion = f32[4096]{0:T(1024)S(1)} fusion(f32[2048]{0:T(1024)S(1)} %reshape.116, s32[4096]{0:T(1024)S(1)} %get-tuple-element.27), kind=kCustom, calls=%fused_computation | custom fusion | bytes 49152 | tf_op jit(solution)/shard_map/jit(_take)/gather | solution.py:12
  42.9 18.2 %gather_fusion.1 = bf16[4096,1024]{1,0:T(8,128)(2,1)} fusion(bf16[256,1024]{1,0:T(8,128)(2,1)S(1)} %copy-done.2, s32[4096]{0:T(1024)S(1)} %get-tuple-element.28), kind=kCustom, calls=%fused_computation.1 | custom fusion | bytes 16793600 | tf_op jit(solution)/shard_map/jit(_take)/gather | solution.py:11
  61.1 7.8 %multiply_convert_fusion = bf16[16,2,1,128,1024]{4,3,1,2,0:T(8,128)(2,1)} fusion(bf16[16,2,1,128,1024]{4,3,1,2,0:T(8,128)(2,1)} %bitcast.47, f32[16,2,128]{2,1,0:T(2,128)S(1)} %bitcast.51, pred[16,2,128]{2,1,0:T(4,128)(4,1)S(1)} %broadcast_in_dim.61), kind=kLoop, calls=%fused_computation.5 | loop fusion | flops 16777216 | bytes 16797696 | tf_op jit(solution)/shard_map/convert_element_type | solution.py:13
  68.9 6.0 %all-to-all-start.1 = ((bf16[16,2,1,128,1024]{4,3,1,2,0:T(8,128)(2,1)}), bf16[16,2,1,128,1024]{4,3,1,2,0:T(8,128)(2,1)}, u32[]{:S(2)}, u32[]{:S(2)}) async-start(bf16[16,2,1,128,1024]{4,3,1,2,0:T(8,128)(2,1)} %multiply_convert_fusion), calls=%async_computation.1 | async-start | bytes 16777216 | tf_op jit(solution)/shard_map/all_to_all | solution.py:53
  75.1 181.9 %all-to-all-done.1 = bf16[16,2,1,128,1024]{4,3,1,2,0:T(8,128)(2,1)} async-done(((bf16[16,2,1,128,1024]{4,3,1,2,0:T(8,128)(2,1)}), bf16[16,2,1,128,1024]{4,3,1,2,0:T(8,128)(2,1)}, u32[]{:S(2)}, u32[]{:S(2)}) %all-to-all-start.1) | async-done | bytes 8388640 | tf_op jit(solution)/shard_map/all_to_all | solution.py:53
  257.0 8.2 %copy.55 = bf16[16,2,1,128,1024]{4,3,0,1,2:T(8,128)(2,1)} copy(bf16[16,2,1,128,1024]{4,3,1,2,0:T(8,128)(2,1)} %all-to-all-done.1) | data formatting | bytes 16777216 | tf_op jit(solution)/shard_map/all_to_all | solution.py:53
  265.2 13.0 %fusion.3 = (bf16[2,2048,512]{2,1,0:T(8,128)(2,1)S(1)}, bf16[2,2048,512]{2,1,0:T(8,128)(2,1)}) fusion(bf16[2,2048,512]{2,1,0:T(8,128)(2,1)} %param.20, bf16[2,2048,512]{2,1,0:T(8,128)(2,1)} %param.19, bf16[2,512,1024]{2,1,0:T(8,128)(2,1)S(1)} %copy-done, bf16[2,2048,1024]{2,1,0:T(8,128)(2,1)} %bitcast.48, pred[2,2048]{1,0:T(4,128)(4,1)S(1)} %bitcast_compare_fusion), kind=kOutput, calls=%fused_computation.15 | convolution fusion | flops 4328521728 | bytes 27267072 | tf_op jit(solution)/shard_map/erd,efd->erf/dot_general | solution.py:24
  278.2 8.2 %fusion.28 = f32[2,2048,1024]{2,1,0:T(8,128)} fusion(bf16[2,2048,512]{2,1,0:T(8,128)(2,1)S(1)} %get-tuple-element.29, bf16[2,1024,512]{2,1,0:T(8,128)(2,1)S(1)} %copy-done.3), kind=kOutput, calls=%fused_computation.59 | convolution fusion | flops 4294967296 | bytes 23068672 | tf_op jit(solution)/shard_map/erf,edf->erd/dot_general | solution.py:36
  286.5 13.0 %add_convert_fusion = bf16[2,2048,1024]{2,1,0:T(8,128)(2,1)} fusion(f32[2,2048,1024]{2,1,0:T(8,128)} %fusion.28, bf16[2,1024,512]{2,1,0:T(8,128)(2,1)S(1)} %copy-done.4, bf16[2,2048,512]{2,1,0:T(8,128)(2,1)} %get-tuple-element.30, bf16[2,2048,512]{2,1,0:T(8,128)(2,1)} %param.19), kind=kOutput, calls=%fused_computation.4 | convolution fusion | flops 4320133120 | bytes 35651584 | tf_op jit(solution)/shard_map/erf,edf->erd/dot_general | solution.py:36
  299.5 8.2 %copy.56 = bf16[1,2,16,128,1024]{4,3,1,0,2:T(8,128)(2,1)} copy(bf16[1,2,16,128,1024]{4,3,2,1,0:T(8,128)(2,1)} %bitcast.50) | data formatting | bytes 16777216 | tf_op jit(solution)/shard_map/broadcast_in_dim;reshape | solution.py:58
  307.7 5.3 %all-to-all-start.2 = ((bf16[1,2,16,128,1024]{4,3,1,0,2:T(8,128)(2,1)}), bf16[1,2,16,128,1024]{4,3,1,0,2:T(8,128)(2,1)}, u32[]{:S(2)}, u32[]{:S(2)}) async-start(bf16[1,2,16,128,1024]{4,3,1,0,2:T(8,128)(2,1)} %copy.56), calls=%async_computation.2 | async-start | bytes 16777216 | tf_op jit(solution)/shard_map/all_to_all | solution.py:58
  313.2 4.5 fusion.16
  318.4 11.1 %convolution_bitcast_fusion.1 = f32[2,1024,512]{1,2,0:T(8,128)} fusion(bf16[2,2048,512]{2,1,0:T(8,128)(2,1)} %copy-done.5, bf16[2,2048,1024]{2,1,0:T(8,128)(2,1)} %param.18), kind=kOutput, calls=%fused_computation.30 | convolution fusion | flops 4294967296 | bytes 16777216 | tf_op jit(solution)/shard_map/erd,erf->edf/dot_general | solution.py:34
  329.5 5.4 %copy.60 = f32[2,1024,512]{2,1,0:T(8,128)} copy(f32[2,1024,512]{1,2,0:T(8,128)} %convolution_bitcast_fusion.1) | data formatting | bytes 8388608
  334.9 12.6 %convolution_bitcast_fusion = f32[2,1024,512]{1,2,0:T(8,128)} fusion(bf16[2,2048,1024]{2,1,0:T(8,128)(2,1)} %param.18, bf16[2,2048,512]{2,1,0:T(8,128)(2,1)} %get-tuple-element.30, bf16[2,2048,512]{2,1,0:T(8,128)(2,1)} %param.19), kind=kOutput, calls=%fused_computation.29 | convolution fusion | flops 4311744512 | bytes 20971520 | tf_op jit(solution)/shard_map/erd,erf->edf/dot_general | solution.py:35
  347.5 5.4 %copy.61 = f32[2,1024,512]{2,1,0:T(8,128)} copy(f32[2,1024,512]{1,2,0:T(8,128)} %convolution_bitcast_fusion) | data formatting | bytes 8388608
  352.8 10.5 %fusion.9 = f32[2,512,1024]{2,1,0:T(8,128)} fusion(bf16[2,2048,1024]{2,1,0:T(8,128)(2,1)} %bitcast.49, pred[2,2048]{1,0:T(4,128)(4,1)S(1)} %bitcast_compare_fusion, bf16[2,2048,512]{2,1,0:T(8,128)(2,1)} %param.20, bf16[2,2048,512]{2,1,0:T(8,128)(2,1)} %param.19), kind=kOutput, calls=%fused_computation.22 | convolution fusion | flops 4315938816 | bytes 20975616 | tf_op jit(solution)/shard_map/erf,erd->efd/dot_general | solution.py:33
  363.4 131.7 %all-to-all-done.2 = bf16[1,2,16,128,1024]{4,3,1,0,2:T(8,128)(2,1)} async-done(((bf16[1,2,16,128,1024]{4,3,1,0,2:T(8,128)(2,1)}), bf16[1,2,16,128,1024]{4,3,1,0,2:T(8,128)(2,1)}, u32[]{:S(2)}, u32[]{:S(2)}) %all-to-all-start.2) | async-done | bytes 8388640 | tf_op jit(solution)/shard_map/all_to_all | solution.py:58
  495.1 15.6 %gather_fusion.2 = bf16[2048,1024]{1,0:T(8,128)(2,1)} fusion(bf16[4096,1024]{1,0:T(8,128)(2,1)} %bitcast.15, s32[2048]{0:T(1024)S(1)} %broadcast_clamp_fusion.1), kind=kCustom, calls=%fused_computation.2 | custom fusion | bytes 8396800 | tf_op jit(solution)/shard_map/jit(_take)/gather | solution.py:19
  510.7 4.9 fusion.12
  (32 shorter events, 3.4 us)
Async XLA Ops:
  0.6 264.6 %copy-start = (bf16[2,512,1024]{2,1,0:T(8,128)(2,1)S(1)}, bf16[2,512,1024]{2,1,0:T(8,128)(2,1)}, u32[]{:S(2)}) copy-start(bf16[2,512,1024]{2,1,0:T(8,128)(2,1)} %param.23) | copy-start | bytes 6291460
  3.3 65.6 %all-to-all-start = ((s32[16,2,1]{1,2,0:T(1,128)}), s32[16,2,1]{1,2,0:T(1,128)S(1)}, u32[]{:S(2)}, u32[]{:S(2)}) async-start(s32[16,2,1]{1,2,0:T(1,128)} %bitcast.1), calls=%async_computation | async-start | bytes 16384 | tf_op jit(solution)/shard_map/all_to_all | solution.py:54
  19.8 23.1 %copy-start.2 = (bf16[256,1024]{1,0:T(8,128)(2,1)S(1)}, bf16[256,1024]{1,0:T(8,128)(2,1)}, u32[]{:S(2)}) copy-start(bf16[256,1024]{1,0:T(8,128)(2,1)} %param.12) | copy-start | bytes 1572868
  68.9 188.1 %all-to-all-start.1 = ((bf16[16,2,1,128,1024]{4,3,1,2,0:T(8,128)(2,1)}), bf16[16,2,1,128,1024]{4,3,1,2,0:T(8,128)(2,1)}, u32[]{:S(2)}, u32[]{:S(2)}) async-start(bf16[16,2,1,128,1024]{4,3,1,2,0:T(8,128)(2,1)} %multiply_convert_fusion), calls=%async_computation.1 | async-start | bytes 16777216 | tf_op jit(solution)/shard_map/all_to_all | solution.py:53
  265.2 13.0 %copy-start.3 = (bf16[2,1024,512]{2,1,0:T(8,128)(2,1)S(1)}, bf16[2,1024,512]{2,1,0:T(8,128)(2,1)}, u32[]{:S(2)}) copy-start(bf16[2,1024,512]{2,1,0:T(8,128)(2,1)} %param.21) | copy-start | bytes 6291460
  278.2 8.3 %copy-start.5 = (bf16[2,2048,512]{2,1,0:T(8,128)(2,1)}, bf16[2,2048,512]{2,1,0:T(8,128)(2,1)S(1)}, u32[]{:S(2)}) copy-start(bf16[2,2048,512]{2,1,0:T(8,128)(2,1)S(1)} %get-tuple-element.29) | copy-start | bytes 12582916
  278.2 8.3 %copy-start.4 = (bf16[2,1024,512]{2,1,0:T(8,128)(2,1)S(1)}, bf16[2,1024,512]{2,1,0:T(8,128)(2,1)}, u32[]{:S(2)}) copy-start(bf16[2,1024,512]{2,1,0:T(8,128)(2,1)} %param.22) | copy-start | bytes 6291460
  307.7 187.4 %all-to-all-start.2 = ((bf16[1,2,16,128,1024]{4,3,1,0,2:T(8,128)(2,1)}), bf16[1,2,16,128,1024]{4,3,1,0,2:T(8,128)(2,1)}, u32[]{:S(2)}, u32[]{:S(2)}) async-start(bf16[1,2,16,128,1024]{4,3,1,0,2:T(8,128)(2,1)} %copy.56), calls=%async_computation.2 | async-start | bytes 16777216 | tf_op jit(solution)/shard_map/all_to_all | solution.py:58
  495.1 20.5 %copy-start.1 = (bf16[2,512,1024]{2,1,0:T(8,128)(2,1)S(1)}, bf16[2,512,1024]{2,1,0:T(8,128)(2,1)}, u32[]{:S(2)}) copy-start(bf16[2,512,1024]{2,1,0:T(8,128)(2,1)} %param.23) | copy-start | bytes 6291460
where the time goes:
time: 517 us; the launch traced here: 516 us
  waiting for transfers between devices  314 us (61%)
  local copies, waits for them, and re-layouts  95.4 us (18%)
  matrix products  73.1 us (14%)
  starting transfers between devices  17.8 us (3%)
  other arithmetic  15 us (3%)
    all_to_all x1, waiting for transfers between devices, local_step(): lax.all_to_all(send_rows.reshape(n_dev, n_loc, cap_rows, model_dim), 'ep'...  182 us
    all_to_all x1, waiting for transfers between devices, local_step(): lax.all_to_all(grad_disp.reshape(n_loc, n_dev, cap_rows, model_dim), 'ep'...  132 us
    gather x1, local copies, waits for them, and re-layouts, build_send(): jnp.take(gate_vals.reshape(-1), row_source, mode='fill', fill_value=0)  23 us
    gather x1, local copies, waits for them, and re-layouts, build_send(): jnp.take(grad_y, row_source // top_k, axis=0, mode='fill', fill_value=0)  18.2 us
    gather x1, local copies, waits for them, and re-layouts, gather_back(): jnp.take(ret_rows, src_row, axis=0, mode='fill', fill_value=0)  15.6 us
    dot_general x1, matrix products, expert_grads(): jnp.einsum('erf,edf->erd', grad_hup, w_up, preferred_element_type=jnp.flo...  13 us
    dot_general x1, matrix products, expert_grads(): jnp.einsum('erd,efd->erf', grad_rows, w_down, preferred_element_type=jnp....  13 us
    dot_general x1, matrix products, expert_grads(): jnp.einsum('erd,erf->edf', x_rows, grad_hup, preferred_element_type=jnp.f...  12.6 us
  transfers between devices with their start and end apart: 3, of which 2 were waited for; matrix products, arithmetic and copies ran while one was open for 21% of the time, Pallas kernels for 0%

commit v1 on v0

v1 whole, which is shorter than its diff:
```python
import jax
import jax.numpy as jnp
from jax import lax
from jax.sharding import PartitionSpec as P

F32 = jnp.float32
BF16 = jnp.bfloat16


def routing_tables(gate_vals, topk_idx, slot_ids, pair_counts):
    n_exp = pair_counts.shape[1]
    hit = topk_idx[None] == lax.broadcasted_iota(jnp.int32, (n_exp, 1, 1), 0)
    slot = jnp.max(jnp.where(hit, slot_ids[None], -1), axis=2)
    gate = jnp.sum(jnp.where(hit, gate_vals[None], 0.0), axis=2)
    slot = jnp.where(slot < pair_counts.reshape(n_exp, 1), slot, -1)
    return slot, gate


def solution(mesh):
    n_dev = mesh.shape["ep"]
    rows_spec = P(("dp", "ep"), None)
    cube_spec = P(("dp", "ep"), None, None)
    weight_spec = P("ep", None, None)

    def local_step(grad_y, gate_vals, topk_idx, slot_ids, pair_counts, y_routed, x_disp, h_gate, h_up, w_gate, w_up, w_down):
        n_loc = w_gate.shape[0]
        cap_rows = x_disp.shape[1] // n_dev
        tok, model_dim = grad_y.shape
        all_y = lax.all_gather(grad_y, "ep")
        slot, gate = routing_tables(gate_vals, topk_idx, slot_ids, pair_counts)
        meta = jnp.stack([slot.astype(F32), gate], axis=1).reshape(n_dev, n_loc, 2, tok)
        meta = lax.all_to_all(meta, "ep", 0, 0)
        grad_gate = jnp.einsum("td,tkd->tk", grad_y, y_routed, preferred_element_type=F32)
        hot = meta[:, :, 0][:, :, None, :] == lax.broadcasted_iota(jnp.int32, (1, 1, cap_rows, 1), 2).astype(F32)
        gate_rows = jnp.sum(jnp.where(hot, meta[:, :, 1][:, :, None, :], 0.0), axis=3)
        pick = hot.astype(BF16)
        rows = jnp.einsum("sect,std->escd", pick, all_y, preferred_element_type=F32)
        grad_rows = (rows * jnp.transpose(gate_rows, (1, 0, 2))[..., None]).astype(BF16).reshape(n_loc, n_dev * cap_rows, model_dim)
        grad_h = jnp.einsum("erd,efd->erf", grad_rows, w_down, preferred_element_type=F32).astype(BF16).astype(F32)
        gate_f = h_gate.astype(F32)
        up_f = h_up.astype(F32)
        sig = jax.nn.sigmoid(gate_f)
        act = gate_f * sig
        hidden = (act * up_f).astype(BF16)
        d_gate = (grad_h * up_f * sig * (1.0 + gate_f * (1.0 - sig))).astype(BF16)
        d_up = (grad_h * act).astype(BF16)
        ret = (jnp.einsum("erf,edf->erd", d_gate, w_gate, preferred_element_type=F32) + jnp.einsum("erf,edf->erd", d_up, w_up, preferred_element_type=F32)).astype(BF16)
        part = jnp.einsum("sect,escd->std", pick, ret.reshape(n_loc, n_dev, cap_rows, model_dim), preferred_element_type=F32)
        grad_x = lax.psum_scatter(part.reshape(n_dev * tok, model_dim), "ep", scatter_dimension=0, tiled=True).astype(BF16)
        grad_wdown = jnp.einsum("erf,erd->efd", hidden, grad_rows, preferred_element_type=F32)
        grad_wgate = jnp.einsum("erd,erf->edf", x_disp, d_gate, preferred_element_type=F32)
        grad_wup = jnp.einsum("erd,erf->edf", x_disp, d_up, preferred_element_type=F32)
        return grad_x, grad_gate, grad_wgate, grad_wup, grad_wdown

    return jax.shard_map(local_step, mesh=mesh, in_specs=(rows_spec, rows_spec, rows_spec, rows_spec, rows_spec, cube_spec, cube_spec, cube_spec, cube_spec, weight_spec, weight_spec, weight_spec), out_specs=(rows_spec, rows_spec, cube_spec, cube_spec, cube_spec), check_vma=False)
```

time: 517 us -> 333 us (0.64)
  waiting for transfers between devices: 314 us -> 184 us
  local copies, waits for them, and re-layouts: 95.4 us -> 21.3 us
  matrix products: 73.1 us -> 95.5 us
  between operations: 0.78 us -> 14.1 us
  starting transfers between devices: 17.8 us -> 6.54 us
  other arithmetic: 15 us -> 8.28 us
    all_to_all x3 -> x1, waiting for transfers between devices: 314 us -> 4.28 us  [local_step(): meta = lax.all_to_all(meta, 'ep', 0, 0)]
    reduce_scatter x0 -> x1, waiting for transfers between devices: none -> 120 us  [local_step(): lax.psum_scatter(part.reshape(n_dev * tok, model_dim), 'ep', scatter_dime...]
    all_gather x0 -> x1, waiting for transfers between devices: none -> 59.6 us  [local_step(): all_y = lax.all_gather(grad_y, 'ep')]
    gather x3 -> x0, local copies, waits for them, and re-layouts: 56.8 us -> none  [the longest x1 23 us: build_send(): jnp.take(gate_vals.reshape(-1), row_source, mode='fill', fill_value=0)]
    dot_general x7 -> x9, matrix products: 73.1 us -> 95.5 us  [the longest x1 14.1 us: local_step(): jnp.einsum('erd,efd->erf', grad_rows, w_down, preferred_element_type=F32)]
    all_to_all x3 -> x1, starting transfers between devices: 17.8 us -> 6.47 us  [local_step(): meta = lax.all_to_all(meta, 'ep', 0, 0)]
    another operation x2 -> x1, local copies, waits for them, and re-layouts: 8.88 us -> 0.02 us  [local_step(): jnp.stack([slot.astype(F32), gate], axis=1).reshape(n_dev, n_loc, 2, tok)]
    all_to_all x2 -> x0, local copies, waits for them, and re-layouts: 8.29 us -> none  [the longest x1 8.21 us: local_step(): lax.all_to_all(send_rows.reshape(n_dev, n_loc, cap_rows, model_dim), 'ep'...]
  transfers between devices with their start and end apart: 3 -> 3, of which waited for: 2 -> 3; matrix products, arithmetic and copies ran while one was open for 21% -> 18% of each run, Pallas kernels for 0% -> 0%
where the time goes in v1:
time: 333 us; the launch traced here: 330 us
  waiting for transfers between devices  184 us (55%)
  matrix products  95.5 us (29%)
  local copies, waits for them, and re-layouts  21.3 us (6%)
  between operations  14.1 us (4%)
  other arithmetic  8.28 us (2%)
  starting transfers between devices  6.54 us (2%)
    reduce_scatter x1, waiting for transfers between devices, local_step(): lax.psum_scatter(part.reshape(n_dev * tok, model_dim), 'ep', scatter_dime...  120 us
    all_gather x1, waiting for transfers between devices, local_step(): all_y = lax.all_gather(grad_y, 'ep')  59.6 us
    dot_general x1, matrix products, local_step(): jnp.einsum('erd,efd->erf', grad_rows, w_down, preferred_element_type=F32)  14.1 us
    dot_general x1, matrix products, local_step(): jnp.einsum('erf,edf->erd', d_up, w_up, preferred_element_type=F32)  13.2 us
    dot_general x1, matrix products, local_step(): jnp.einsum('erf,erd->efd', hidden, grad_rows, preferred_element_type=F32)  12.8 us
    dot_general x1, matrix products, local_step(): jnp.einsum('erd,erf->edf', x_disp, d_up, preferred_element_type=F32)  12.6 us
    unnamed x15, local copies, waits for them, and re-layouts  12.3 us
    dot_general x1, matrix products, local_step(): jnp.einsum('erd,erf->edf', x_disp, d_gate, preferred_element_type=F32)  11.1 us
  transfers between devices with their start and end apart: 3, of which 3 were waited for; matrix products, arithmetic and copies ran while one was open for 18% of the time, Pallas kernels for 0%

profile of v1, /device:TPU:19, one launch (start us, length us, event | category | flops | bytes accessed | tf_op | source)
XLA Modules:
  0.0 330.0 jit_solution(14126874144518275254)
XLA Ops:
  7.2 0.7 all-gather.3.cloned.1.call-update
  7.9 0.8 select_reduce_fusion.1
  9.3 1.3 reduce.3
  10.7 0.8 select_reduce_fusion
  12.3 6.5 %all-to-all-start = ((f32[16,2,2,256]{3,1,2,0:T(2,128)}), f32[16,2,2,256]{3,1,2,0:T(2,128)S(1)}, u32[]{:S(2)}, u32[]{:S(2)}) async-start(f32[16,2,2,256]{3,1,2,0:T(2,128)} %pad_maximum_fusion), calls=%async_computation | async-start | bytes 131072 | tf_op jit(solution)/shard_map/all_to_all | solution.py:32
  18.8 4.3 %all-to-all-done = f32[16,2,2,256]{3,1,2,0:T(2,128)S(1)} async-done(((f32[16,2,2,256]{3,1,2,0:T(2,128)}), f32[16,2,2,256]{3,1,2,0:T(2,128)S(1)}, u32[]{:S(2)}, u32[]{:S(2)}) %all-to-all-start) | async-done | bytes 65568 | tf_op jit(solution)/shard_map/all_to_all | solution.py:32
  23.1 2.5 fusion.14
  25.6 59.6 %all-gather.3.cloned.1.call-done = bf16[4096,1024]{1,0:T(8,128)(2,1)} async-done(((bf16[256,1024]{1,0:T(8,128)(2,1)}), bf16[4096,1024]{1,0:T(8,128)(2,1)}) %all-gather.3.cloned.1.call-update) | async-done | bytes 8388624 | tf_op jit(solution)/shard_map/all_gather | solution.py:29
  85.2 9.5 %fusion = bf16[2,16,128,1024]{3,2,0,1:T(8,128)(2,1)} fusion(bf16[16,256,1024,1]{2,1,3,0:T(8,128)(2,1)} %bitcast.43, f32[2,16,128]{2,0,1:T(2,128)S(1)} %bitcast.48, f32[128]{0:T(128)S(1)} %iota_convert_fusion, f32[16,2,256]{2,1,0:T(2,128)S(1)} %get-tuple-element.25), kind=kOutput, calls=%fused_computation.1 | convolution fusion | flops 2156920832 | bytes 16826880 | tf_op jit(solution)/shard_map/sect,std->escd/dot_general | solution.py:37
  94.7 8.2 %copy.53 = bf16[2,16,128,1024]{3,2,1,0:T(8,128)(2,1)} copy(bf16[2,16,128,1024]{3,2,0,1:T(8,128)(2,1)} %fusion) | data formatting | bytes 16777216 | tf_op jit(solution)/shard_map/convert_element_type | solution.py:38
  102.9 14.1 %fusion.4 = (bf16[2,2048,512]{2,1,0:T(8,128)(2,1)S(1)}, bf16[2,2048,512]{2,1,0:T(8,128)(2,1)}) fusion(bf16[2,2048,512]{2,1,0:T(8,128)(2,1)} %param.20, bf16[2,2048,512]{2,1,0:T(8,128)(2,1)} %param.19, bf16[2,2048,1024]{2,1,0:T(8,128)(2,1)} %bitcast.44, bf16[2,512,1024]{2,1,0:T(8,128)(2,1)S(1)} %copy-done), kind=kOutput, calls=%fused_computation.12 | convolution fusion | flops 4324327424 | bytes 27262976 | tf_op jit(solution)/shard_map/erd,efd->erf/dot_general | solution.py:39
  117.0 8.1 %fusion.27 = f32[2,2048,1024]{2,1,0:T(8,128)} fusion(bf16[2,2048,512]{2,1,0:T(8,128)(2,1)S(1)} %get-tuple-element.27, bf16[2,1024,512]{2,1,0:T(8,128)(2,1)S(1)} %copy-done.3), kind=kOutput, calls=%fused_computation.44 | convolution fusion | flops 4294967296 | bytes 23068672 | tf_op jit(solution)/shard_map/erf,edf->erd/dot_general | solution.py:47
  125.2 13.2 %add_convert_fusion = bf16[2,2048,1024]{2,1,0:T(8,128)(2,1)} fusion(f32[2,2048,1024]{2,1,0:T(8,128)} %fusion.27, bf16[2,1024,512]{2,1,0:T(8,128)(2,1)S(1)} %copy-done.4, bf16[2,2048,512]{2,1,0:T(8,128)(2,1)} %get-tuple-element.28, bf16[2,2048,512]{2,1,0:T(8,128)(2,1)} %param.19), kind=kOutput, calls=%fused_computation.2 | convolution fusion | flops 4320133120 | bytes 35651584 | tf_op jit(solution)/shard_map/erf,edf->erd/dot_general | solution.py:47
  138.4 9.2 %fusion.10 = f32[16,256,1024,1]{2,1,3,0:T(8,128)} fusion(bf16[2,16,128,1024]{3,2,1,0:T(8,128)(2,1)} %bitcast.42, f32[128]{0:T(128)S(1)} %iota_convert_fusion, f32[16,2,256]{2,1,0:T(2,128)S(1)} %get-tuple-element.25), kind=kOutput, calls=%fused_computation.18 | convolution fusion | flops 2148532224 | bytes 25199104 | tf_op jit(solution)/shard_map/sect,escd->std/dot_general | solution.py:48
  147.7 1.0 copy-done.2
  148.7 4.8 %fusion.21 = f32[256,1,8]{2,1,0:T(1,128)S(1)} fusion(bf16[256,8,1024]{2,1,0:T(8,128)(2,1)} %param.17, bf16[256,1024,1]{1,0,2:T(8,128)(2,1)S(1)} %bitcast.46), kind=kOutput, calls=%fused_computation.32 | convolution fusion | flops 4194304 | bytes 4726784 | tf_op jit(solution)/shard_map/td,tkd->tk/dot_general | solution.py:33
  153.5 0.7 copy.64
  154.2 11.1 %convolution_bitcast_fusion.1 = f32[2,1024,512]{1,2,0:T(8,128)} fusion(bf16[2,2048,512]{2,1,0:T(8,128)(2,1)} %copy-done.5, bf16[2,2048,1024]{2,1,0:T(8,128)(2,1)} %param.18), kind=kOutput, calls=%fused_computation.27 | convolution fusion | flops 4294967296 | bytes 16777216 | tf_op jit(solution)/shard_map/erd,erf->edf/dot_general | solution.py:51
  165.3 5.4 %copy.58 = f32[2,1024,512]{2,1,0:T(8,128)} copy(f32[2,1024,512]{1,2,0:T(8,128)} %convolution_bitcast_fusion.1) | data formatting | bytes 8388608
  170.7 12.6 %convolution_bitcast_fusion = f32[2,1024,512]{1,2,0:T(8,128)} fusion(bf16[2,2048,1024]{2,1,0:T(8,128)(2,1)} %param.18, bf16[2,2048,512]{2,1,0:T(8,128)(2,1)} %get-tuple-element.28, bf16[2,2048,512]{2,1,0:T(8,128)(2,1)} %param.19), kind=kOutput, calls=%fused_computation.26 | convolution fusion | flops 4311744512 | bytes 20971520 | tf_op jit(solution)/shard_map/erd,erf->edf/dot_general | solution.py:52
  183.3 5.4 %copy.59 = f32[2,1024,512]{2,1,0:T(8,128)} copy(f32[2,1024,512]{1,2,0:T(8,128)} %convolution_bitcast_fusion) | data formatting | bytes 8388608
  188.6 12.8 %fusion.15 = f32[2,512,1024]{2,1,0:T(8,128)} fusion(bf16[2,2048,1024]{2,1,0:T(8,128)(2,1)} %bitcast.45, bf16[2,2048,512]{2,1,0:T(8,128)(2,1)} %param.20, bf16[2,2048,512]{2,1,0:T(8,128)(2,1)} %param.19), kind=kOutput, calls=%fused_computation.24 | convolution fusion | flops 4311744512 | bytes 20971520 | tf_op jit(solution)/shard_map/erf,erd->efd/dot_general | solution.py:50
  201.4 119.6 %reduce-scatter.2.cloned.1.call-done = f32[256,1024]{1,0:T(8,128)} async-done(((f32[4096,1024]{1,0:T(8,128)}), f32[256,1024]{1,0:T(8,128)}) %reduce-scatter.2.cloned.1.call-update) | async-done | bytes 1048592 | tf_op jit(solution)/shard_map/reduce_scatter | solution.py:49
  321.0 2.1 convert_element_type.60
  (22 shorter events, 1.5 us)
Async XLA Ops:
  7.2 95.8 %copy-start = (bf16[2,512,1024]{2,1,0:T(8,128)(2,1)S(1)}, bf16[2,512,1024]{2,1,0:T(8,128)(2,1)}, u32[]{:S(2)}) copy-start(bf16[2,512,1024]{2,1,0:T(8,128)(2,1)} %param.23) | copy-start | bytes 6291460
  7.2 78.0 %all-gather.3.cloned.1.call-start = ((), (), s32[]{:S(2)}) async-start(), calls=%async_computation.3 | async-start | bytes 8912896 | tf_op jit(solution)/shard_map/all_gather | solution.py:29
  12.3 10.8 %all-to-all-start = ((f32[16,2,2,256]{3,1,2,0:T(2,128)}), f32[16,2,2,256]{3,1,2,0:T(2,128)S(1)}, u32[]{:S(2)}, u32[]{:S(2)}) async-start(f32[16,2,2,256]{3,1,2,0:T(2,128)} %pad_maximum_fusion), calls=%async_computation | async-start | bytes 131072 | tf_op jit(solution)/shard_map/all_to_all | solution.py:32
  18.7 302.3 %reduce-scatter.2.cloned.1.call-start = ((), (), s32[]{:S(2)}) async-start(), calls=%async_computation.2 | async-start | bytes 17825792 | tf_op jit(solution)/shard_map/reduce_scatter | solution.py:49
  102.9 14.1 %copy-start.3 = (bf16[2,1024,512]{2,1,0:T(8,128)(2,1)S(1)}, bf16[2,1024,512]{2,1,0:T(8,128)(2,1)}, u32[]{:S(2)}) copy-start(bf16[2,1024,512]{2,1,0:T(8,128)(2,1)} %param.21) | copy-start | bytes 6291460
  117.0 8.1 %copy-start.5 = (bf16[2,2048,512]{2,1,0:T(8,128)(2,1)}, bf16[2,2048,512]{2,1,0:T(8,128)(2,1)S(1)}, u32[]{:S(2)}) copy-start(bf16[2,2048,512]{2,1,0:T(8,128)(2,1)S(1)} %get-tuple-element.27) | copy-start | bytes 12582916
  117.0 8.1 %copy-start.4 = (bf16[2,1024,512]{2,1,0:T(8,128)(2,1)S(1)}, bf16[2,1024,512]{2,1,0:T(8,128)(2,1)}, u32[]{:S(2)}) copy-start(bf16[2,1024,512]{2,1,0:T(8,128)(2,1)} %param.22) | copy-start | bytes 6291460
  147.6 1.0 copy-start.2
  188.6 134.5 %copy-start.1 = (bf16[2,512,1024]{2,1,0:T(8,128)(2,1)S(1)}, bf16[2,512,1024]{2,1,0:T(8,128)(2,1)}, u32[]{:S(2)}) copy-start(bf16[2,512,1024]{2,1,0:T(8,128)(2,1)} %param.23) | copy-start | bytes 6291460
Sparse Core Ops, SparseCore 0:
  10.2 75.0 all-gather.2
  147.8 173.1 reduce-scatter.1

commit v2 on v1

v2 whole, which is shorter than its diff:
```python
import jax
import jax.numpy as jnp
from jax import lax
from jax.experimental import pallas as pl
from jax.experimental.pallas import tpu as pltpu
from jax.sharding import PartitionSpec as P

F32 = jnp.float32
BF16 = jnp.bfloat16
VMEM = pltpu.VMEM
DMA = pltpu.SemaphoreType.DMA
ANY = pl.BlockSpec(memory_space=pl.ANY)
VM = pl.BlockSpec(memory_space=pltpu.VMEM)


def position():
    me = lax.axis_index("ep")
    return me, me // 4, (me // 2) % 2, me % 2


def near_first(z, k):
    m = z // 2
    zz = z + m * (3 - 2 * z)
    v = (zz, 1 - zz, 2, 3)[k]
    return v + m * (3 - 2 * v)


def far_first(z, k):
    m = z // 2
    zz = z + m * (3 - 2 * z)
    v = 3 - k + zz * jnp.where(k == 1, -2, jnp.where(k >= 2, 1, 0))
    return v + m * (3 - 2 * v)


def dot_nt(a, b):
    return lax.dot_general(a, b, (((1,), (1,)), ((), ())), preferred_element_type=F32)


def dot_tn(a, b):
    return lax.dot_general(a, b, (((0,), (0,)), ((), ())), preferred_element_type=F32)


def one_hot(slot, cap):
    return slot == lax.broadcasted_iota(jnp.int32, (cap, slot.shape[1]), 0).astype(F32)


def gather_kernel(gy, meta_out, hg_hbm, hu_hbm, wd_hbm, dh1_hbm, dh3_hbm, gwd_hbm, meta_res, tok, meta, hg, hu, wd, d_ref, a_ref, dh1, dh3, acc, ld_sem, st_sem, send, recv, m_send, m_recv):
    me, z, y, c = position()
    cap = d_ref.shape[0] // 2
    sib = me + 1 - 2 * c
    ynb = me + 2 - 4 * y
    end = (z == 0) | (z == 3)
    loads = [pltpu.make_async_copy(s, d, ld_sem.at[i]) for i, (s, d) in enumerate(((wd_hbm, wd), (hg_hbm, hg), (hu_hbm, hu)))]
    for cp in loads:
        cp.start()
    barrier = pltpu.get_barrier_semaphore()
    for k in range(1, 16):
        pl.semaphore_signal(barrier, inc=1, device_id={"ep": (me + k) % 16})
    pl.semaphore_wait(barrier, 15)

    def put(src, slot, way, to):
        return pltpu.make_async_remote_copy(src_ref=src, dst_ref=tok.at[slot], send_sem=send.at[slot, way], recv_sem=recv.at[slot], device_id={"ep": to})

    started = []

    def go(src, slot, way, to, cond=None):
        cp = put(src, slot, way, to)
        if cond is None:
            cp.start()
        else:
            pl.when(cond)(cp.start)
        started.append((cp, cond))

    def arrive(slot):
        put(tok.at[slot], slot, 0, me).wait_recv()

    def meta_copy(k):
        to = (me + k) % 16
        return pltpu.make_async_remote_copy(src_ref=meta_out.at[to // 2], dst_ref=meta.at[me], send_sem=m_send.at[k], recv_sem=m_recv.at[me], device_id={"ep": to})

    go(gy, me, 3, sib)
    for k in range(1, 16):
        meta_copy(k).start()
    go(gy, me, 0, (me + 4) % 16, z < 3)
    go(gy, me, 1, (me + 12) % 16, z > 0)
    go(gy, me, 2, ynb)
    tok[me] = gy[...]
    meta[me] = meta_out[me // 2]
    acc[...] = jnp.zeros_like(acc)
    for k in range(1, 16):
        src = (me + k) % 16
        pltpu.make_async_remote_copy(src_ref=meta_out.at[0], dst_ref=meta.at[src], send_sem=m_send.at[k], recv_sem=m_recv.at[src], device_id={"ep": src}).wait_recv()
    for cp in loads:
        cp.wait()

    def slot_of(zs, ys, cs):
        return zs * 4 + ys * 2 + cs

    def relay(k, cond=None):
        zs = near_first(z, k)
        slot = slot_of(zs, y, c)
        away = jnp.where(zs < z, 1, -1)
        nz = z + away
        inside = (nz >= 0) & (nz <= 3)

        def body():
            arrive(slot)
            pl.when(inside)(put(tok.at[slot], slot, 0, (me + 4 * away + 16) % 16).start)
            put(tok.at[slot], slot, 2, ynb).start()
            put(tok.at[slot], slot, 3, sib).start()

        body() if cond is None else pl.when(cond)(body)

    def y_arrival(k):
        slot = slot_of(near_first(z, k), 1 - y, c)
        arrive(slot)
        go(tok.at[slot], slot, 3, sib)

    def compute(zs, ys):
        chip = zs * 2 + ys
        rows = pl.ds(pl.multiple_of(chip * 2 * cap, 2 * cap), 2 * cap)

        def per_expert(e, _):
            for h in range(2):
                s = chip * 2 + h
                hot = one_hot(meta[s, c * 2 + e], cap)
                gate = jnp.sum(jnp.where(hot, meta[s, 4 + c * 2 + e], 0.0), axis=1, keepdims=True)
                picked = jnp.dot(jnp.where(hot, 1.0, 0.0).astype(BF16), tok[s], preferred_element_type=F32)
                d_ref[h * cap:(h + 1) * cap, :] = (picked * gate).astype(BF16)
            g = dot_nt(d_ref[...], wd[e]).astype(BF16).astype(F32)
            h1 = hg[e, rows, :].astype(F32)
            h3 = hu[e, rows, :].astype(F32)
            sig = jax.nn.sigmoid(h1)
            act = h1 * sig
            a_ref[...] = (act * h3).astype(BF16)
            dh1[e, rows, :] = (g * h3 * sig * (1.0 + h1 * (1.0 - sig))).astype(BF16)
            dh3[e, rows, :] = (g * act).astype(BF16)
            acc[e] += dot_tn(a_ref[...], d_ref[...])
            return 0

        lax.fori_loop(0, 2, per_expert, 0)

    def from_sib(k, ys):
        arrive(slot_of(near_first(z, k), ys, 1 - c))

    from_sib(0, y)
    compute(z, y)
    for phase in range(1, 5):
        if phase < 4:
            if phase == 1:
                relay(1)
                relay(2, jnp.logical_not(end))
            elif phase == 2:
                relay(2, end)
                relay(3, jnp.logical_not(end))
            else:
                relay(3, end)
        y_arrival(phase - 1)
        if phase < 4:
            from_sib(phase, y)
        from_sib(phase - 1, 1 - y)
        lo = near_first(z, phase - 1)
        hi = near_first(z, phase) if phase < 4 else lo

        def both(j, _, lo=lo, hi=hi):
            compute(jnp.where(j == 0, hi, lo), jnp.where(j == 0, y, 1 - y))
            return 0

        if phase < 4:
            lax.fori_loop(0, 2, both, 0)
        else:
            compute(lo, 1 - y)

    outs = [pltpu.make_async_copy(s, d, st_sem.at[i]) for i, (s, d) in enumerate(((dh1, dh1_hbm), (dh3, dh3_hbm), (acc, gwd_hbm)))]
    for cp in outs:
        cp.start()
    meta_res[...] = meta[...]
    for cp, cond in started:
        if cond is None:
            cp.wait_send()
        else:
            pl.when(cond)(cp.wait_send)
    for k in range(1, 4):
        zs = near_first(z, k)
        slot = slot_of(zs, y, c)
        nz = z + jnp.where(zs < z, 1, -1)
        pl.when((nz >= 0) & (nz <= 3))(put(tok.at[slot], slot, 0, me).wait_send)
        put(tok.at[slot], slot, 2, ynb).wait_send()
        put(tok.at[slot], slot, 3, sib).wait_send()
    for k in range(1, 16):
        meta_copy(k).wait_send()
    for cp in outs:
        cp.wait()


def return_kernel(meta, dh1_hbm, dh3_hbm, wg_hbm, wu_hbm, x_hbm, gx, gwg_hbm, gwu_hbm, dh1, dh3, wg, wu, x, r_own, r_send, r_recv, y_send, y_recv, tot, z_left, z_right, f_send, f_recv, og, ou, ld_sem, st_sem, rs, rr, ys_sem, yr_sem, zs_sem, zl_sem, zr_sem, fs, fr):
    me, z, y, c = position()
    n_loc, n_rows, ffn = dh1.shape
    cap = n_rows // 16
    half = r_own.shape[3]
    sib = me + 1 - 2 * c
    ynb = me + 2 - 4 * y
    loads = [pltpu.make_async_copy(s, d, ld_sem.at[i]) for i, (s, d) in enumerate(((wg_hbm, wg), (wu_hbm, wu), (dh1_hbm, dh1), (dh3_hbm, dh3), (x_hbm, x)))]
    for cp in loads:
        cp.start()
    barrier = pltpu.get_barrier_semaphore()
    pl.semaphore_signal(barrier, inc=1, device_id={"ep": sib})
    pl.semaphore_signal(barrier, inc=1, device_id={"ep": ynb})

    @pl.when(z > 0)
    def _():
        pl.semaphore_signal(barrier, inc=1, device_id={"ep": (me + 12) % 16})

    @pl.when(z < 3)
    def _():
        pl.semaphore_signal(barrier, inc=1, device_id={"ep": (me + 4) % 16})

    pl.semaphore_wait(barrier, 2 + jnp.where(z > 0, 1, 0) + jnp.where(z < 3, 1, 0))
    for cp in loads[:4]:
        cp.wait()

    def swap(chip):
        return pltpu.make_async_remote_copy(src_ref=r_send.at[chip], dst_ref=r_recv.at[chip], send_sem=rs.at[chip], recv_sem=rr.at[chip], device_id={"ep": sib})

    def y_copy(u):
        return pltpu.make_async_remote_copy(src_ref=y_send.at[u], dst_ref=y_recv.at[u], send_sem=ys_sem.at[u], recv_sem=yr_sem.at[u], device_id={"ep": ynb})

    def to_right(u):
        return pltpu.make_async_remote_copy(src_ref=tot.at[u], dst_ref=z_left.at[u], send_sem=zs_sem.at[u], recv_sem=zl_sem.at[u], device_id={"ep": (me + 4) % 16})

    def to_left(u):
        return pltpu.make_async_remote_copy(src_ref=tot.at[u], dst_ref=z_right.at[u], send_sem=zs_sem.at[u], recv_sem=zr_sem.at[u], device_id={"ep": (me + 12) % 16})

    def last(k=0):
        return pltpu.make_async_remote_copy(src_ref=f_send, dst_ref=f_recv, send_sem=fs.at[0], recv_sem=fr.at[0], device_id={"ep": sib})

    def place(j):
        k, other = j // 2, 1 - j % 2
        return far_first(z, k), y + other * (1 - 2 * y)

    def make_rows(j):
        d, yy = place(j)
        chip = d * 2 + yy
        rows = pl.ds(pl.multiple_of(chip * 2 * cap, 2 * cap), 2 * cap)

        def per_expert(e, _):
            for part, dest in ((1 - c, r_send), (c, r_own)):
                cols = pl.ds(pl.multiple_of(part * half, half), half)
                r = dot_nt(dh1[e, rows, :], wg[e, cols, :]) + dot_nt(dh3[e, rows, :], wu[e, cols, :])
                dest[chip, e] = r.astype(BF16)
            return 0

        lax.fori_loop(0, n_loc, per_expert, 0)
        swap(chip).start()

    def combine(j):
        d, yy = place(j)
        chip = d * 2 + yy
        swap(chip).wait_recv()
        for h in range(2):
            s = chip * 2 + h
            lanes = pl.ds(h * cap, cap)
            ids = (c * 2, c * 2 + 1, 2 - c * 2, 3 - c * 2)
            pick = jnp.concatenate([jnp.where(one_hot(meta[s, i], cap), 1.0, 0.0).astype(BF16) for i in ids], axis=0)
            vals = jnp.concatenate([r_own[chip, 0, lanes, :], r_own[chip, 1, lanes, :], r_recv[chip, 0, lanes, :], r_recv[chip, 1, lanes, :]], axis=0)
            part = dot_tn(pick, vals)
            u = d * 2 + h

            @pl.when(j % 2 == 0)
            def _():
                y_send[u] = part
                y_copy(u).start()

            @pl.when(j % 2 == 1)
            def _():
                tot[u] = part

    def step(j, _):
        @pl.when(j < 8)
        def _():
            make_rows(j)

        @pl.when(j > 0)
        def _():
            combine(j - 1)

        return 0

    lax.fori_loop(0, 9, step, 0)
    loads[4].wait()

    def w_out(i, slot):
        e, t = i // 4, i % 4
        rows = pl.ds(pl.multiple_of(t * og.shape[1], og.shape[1]), og.shape[1])
        return (pltpu.make_async_copy(og.at[slot], gwg_hbm.at[e, rows, :], st_sem.at[slot, 0]),
                pltpu.make_async_copy(ou.at[slot], gwu_hbm.at[e, rows, :], st_sem.at[slot, 1]))

    def weights(i):
        e, t = i // 4, i % 4
        slot = i % 2

        @pl.when(i >= 2)
        def _():
            for cp in w_out(i - 2, slot):
                cp.wait()

        xs = x[e, :, pl.ds(pl.multiple_of(t * og.shape[1], og.shape[1]), og.shape[1])]
        og[slot] = dot_tn(xs, dh1[e])
        ou[slot] = dot_tn(xs, dh3[e])
        for cp in w_out(i, slot):
            cp.start()

    def chain(i, _):
        weights(i)
        d, h = far_first(z, i // 2), i % 2
        u = d * 2 + h
        y_copy(u).wait_recv()
        tot[u] = tot[u] + y_recv[u]

        @pl.when((z <= d) & (z > 0))
        def _():
            to_right(u).wait_recv()
            tot[u] = tot[u] + z_left[u]

        @pl.when((z >= d) & (z < 3))
        def _():
            to_left(u).wait_recv()
            tot[u] = tot[u] + z_right[u]

        @pl.when(z < d)
        def _():
            to_right(u).start()

        @pl.when(z > d)
        def _():
            to_left(u).start()

        @pl.when((z == d) & (h == c))
        def _():
            for k in range(2):
                @pl.when(c == k)
                def _():
                    gx[:, k * half:(k + 1) * half] = tot[u].astype(BF16)

        @pl.when((z == d) & (h != c))
        def _():
            f_send[...] = tot[u].astype(BF16)
            last().start()

        return 0

    lax.fori_loop(0, 8, chain, 0)
    last().wait()
    for k in range(2):
        @pl.when(c == k)
        def _():
            gx[:, (1 - k) * half:(2 - k) * half] = f_recv[...]

    def drain(u, _):
        swap(u).wait_send()
        y_copy(u).wait_send()
        pl.when(z != u // 2)(to_right(u).wait_send)
        return 0

    lax.fori_loop(0, 8, drain, 0)
    for i in (6, 7):
        for cp in w_out(i, i % 2):
            cp.wait()


def routing_tables(gate_vals, topk_idx, slot_ids, pair_counts):
    n_exp = pair_counts.shape[1]
    hit = topk_idx[None] == lax.broadcasted_iota(jnp.int32, (n_exp, 1, 1), 0)
    slot = jnp.max(jnp.where(hit, slot_ids[None], -1), axis=2)
    gate = jnp.sum(jnp.where(hit, gate_vals[None], 0.0), axis=2)
    slot = jnp.where(slot < pair_counts.reshape(n_exp, 1), slot, -1)
    return slot, gate


def solution(mesh):
    rows_spec = P(("dp", "ep"), None)
    cube_spec = P(("dp", "ep"), None, None)
    weight_spec = P("ep", None, None)

    def local_step(grad_y, gate_vals, topk_idx, slot_ids, pair_counts, y_routed, x_disp, h_gate, h_up, w_gate, w_up, w_down):
        n_loc, n_rows, ffn = h_gate.shape
        tok, dim = grad_y.shape
        half = dim // 2
        cap = n_rows // 16
        shape = jax.ShapeDtypeStruct
        slot, gate = routing_tables(gate_vals, topk_idx, slot_ids, pair_counts)
        meta_out = jnp.concatenate([slot.astype(F32).reshape(8, 4, 1, tok), gate.reshape(8, 4, 1, tok)], axis=1)
        dh1, dh3, grad_wdown, meta = pl.pallas_call(
            gather_kernel,
            out_shape=(shape((n_loc, n_rows, ffn), BF16), shape((n_loc, n_rows, ffn), BF16), shape((n_loc, ffn, dim), F32), shape((16, 8, 1, tok), F32)),
            in_specs=[VM, VM, ANY, ANY, ANY],
            out_specs=(ANY, ANY, ANY, VM),
            scratch_shapes=[
                VMEM((16, tok, dim), BF16), VMEM((16, 8, 1, tok), F32),
                VMEM((n_loc, n_rows, ffn), BF16), VMEM((n_loc, n_rows, ffn), BF16), VMEM((n_loc, ffn, dim), BF16),
                VMEM((2 * cap, dim), BF16), VMEM((2 * cap, ffn), BF16),
                VMEM((n_loc, n_rows, ffn), BF16), VMEM((n_loc, n_rows, ffn), BF16), VMEM((n_loc, ffn, dim), F32),
                DMA((3,)), DMA((3,)), DMA((16, 4)), DMA((16,)), DMA((16,)), DMA((16,)),
            ],
            compiler_params=pltpu.CompilerParams(collective_id=1, has_side_effects=True, vmem_limit_bytes=56 << 20),
            name="gather_step",
        )(grad_y, meta_out, h_gate, h_up, w_down)
        grad_gate = jnp.einsum("td,tkd->tk", grad_y, y_routed, preferred_element_type=F32)
        unit = (8, tok, half)
        grad_x, grad_wgate, grad_wup = pl.pallas_call(
            return_kernel,
            out_shape=(shape((tok, dim), BF16), shape((n_loc, dim, ffn), F32), shape((n_loc, dim, ffn), F32)),
            in_specs=[VM, ANY, ANY, ANY, ANY, ANY],
            out_specs=(VM, ANY, ANY),
            scratch_shapes=[
                VMEM((n_loc, n_rows, ffn), BF16), VMEM((n_loc, n_rows, ffn), BF16),
                VMEM((n_loc, dim, ffn), BF16), VMEM((n_loc, dim, ffn), BF16), VMEM((n_loc, n_rows, dim), BF16),
                VMEM((8, n_loc, 2 * cap, half), BF16), VMEM((8, n_loc, 2 * cap, half), BF16), VMEM((8, n_loc, 2 * cap, half), BF16),
                VMEM(unit, F32), VMEM(unit, F32), VMEM(unit, F32), VMEM(unit, F32), VMEM(unit, F32),
                VMEM((tok, half), BF16), VMEM((tok, half), BF16),
                VMEM((2, 256, ffn), F32), VMEM((2, 256, ffn), F32),
                DMA((5,)), DMA((2, 2)), DMA((8,)), DMA((8,)), DMA((8,)), DMA((8,)), DMA((8,)), DMA((8,)), DMA((8,)), DMA((1,)), DMA((1,)),
            ],
            compiler_params=pltpu.CompilerParams(collective_id=2, has_side_effects=True, vmem_limit_bytes=67043328),
            name="return_step",
        )(meta, dh1, dh3, w_gate, w_up, x_disp)
        return grad_x, grad_gate, grad_wgate, grad_wup, grad_wdown

    return jax.shard_map(local_step, mesh=mesh, in_specs=(rows_spec, rows_spec, rows_spec, rows_spec, rows_spec, cube_spec, cube_spec, cube_spec, cube_spec, weight_spec, weight_spec, weight_spec), out_specs=(rows_spec, rows_spec, cube_spec, cube_spec, cube_spec), check_vma=False)
```

time: 333 us -> 195 us (0.59)
  the two profiles are of different devices: /device:TPU:19 before, /device:TPU:0 now
where the time goes in v2:
time: 195 us
  Pallas kernels  173 us (89%)
  local copies, waits for them, and re-layouts  12.7 us (7%)
  matrix products  5.06 us (3%)
  other arithmetic  3.74 us (2%)
    pallas_call x1, Pallas kernels, local_step(): pl.pallas_call(return_kernel, out_shape=(shape((tok, dim), BF16), shape((...  106 us
    pallas_call x1, Pallas kernels, local_step(): pl.pallas_call(gather_kernel, out_shape=(shape((n_loc, n_rows, ffn), BF16...  66.7 us
    unnamed x11, local copies, waits for them, and re-layouts  11.8 us
    dot_general x1, matrix products, local_step(): jnp.einsum('td,tkd->tk', grad_y, y_routed, preferred_element_type=F32)  5.06 us

profile of v2, /device:TPU:0, one launch (start us, length us, event | category | flops | bytes accessed | tf_op | source)
XLA Modules:
  0.0 194.8 jit_solution(4980895369824504365)
XLA Ops:
  0.6 0.8 select_reduce_fusion.1
  1.5 0.5 broadcast.22
  2.0 1.3 reduce.3
  3.3 0.1 lt.17
  3.4 0.1 fusion.2
  3.5 0.8 select_reduce_fusion
  4.4 0.7 pad_maximum_fusion.meta_out
  5.1 66.7 %gather_step.1 = (bf16[2,2048,512]{2,1,0:T(8,128)(2,1)}, bf16[2,2048,512]{2,1,0:T(8,128)(2,1)}, f32[2,512,1024]{2,1,0:T(8,128)}, f32[16,8,1,256]{3,2,1,0:T(1,128)}) custom-call(bf16[256,1024]{1,0:T(8,128)(2,1)} %gy.1, f32[8,8,1,256]{3,2,1,0:T(1,128)} %pad_maximum_fusion.meta_out, bf16[2,2048,512]{2,1,0:T(8,128)(2,1)} %hg_hbm.1, ...), custom_call_target="tpu_custom_call" | custom-call | tf_op jit(solution)/shard_map/gather_step/pallas_call | solution.py:393
  71.8 105.9 %return_step.1 = (bf16[256,1024]{1,0:T(8,128)(2,1)}, f32[2,1024,512]{2,1,0:T(8,128)}, f32[2,1024,512]{2,1,0:T(8,128)}) custom-call(f32[16,8,1,256]{3,2,1,0:T(1,128)} %get-tuple-element.12.meta, bf16[2,2048,512]{2,1,0:T(8,128)(2,1)} %get-tuple-element.13.dh1_hbm, bf16[2,2048,512]{2,1,0:T(8,128)(2,1)} %get-tuple-element.14.dh3_hbm, ...), custom_call_target="tpu_custom_call" | custom-call | tf_op jit(solution)/shard_map/return_step/pallas_call | solution.py:410
  177.7 0.0 copy-start.2
  177.7 5.1 %fusion = f32[256,1,8]{2,1,0:T(1,128)S(1)} fusion(bf16[256,8,1024]{2,1,0:T(8,128)(2,1)} %param.17, bf16[256,1024,1]{1,0,2:T(8,128)(2,1)} %bitcast.3), kind=kOutput, calls=%fused_computation | convolution fusion | flops 4194304 | bytes 4726784 | tf_op jit(solution)/shard_map/td,tkd->tk/dot_general | solution.py:408
  182.8 0.7 copy.24
  183.4 0.0 copy-done.2
  183.4 0.8 copy.31
  184.2 0.0 copy-start.1
  184.2 4.8 %copy.32 = f32[2,1024,512]{2,1,0:T(8,128)} copy(f32[2,1024,512]{2,1,0:T(8,128)} %get-tuple-element.26) | data formatting | bytes 8388608
  189.1 0.0 copy-done.1
  189.1 0.0 copy-start
  189.1 2.1 %copy.33 = f32[2,1024,512]{2,1,0:T(8,128)} copy(f32[2,1024,512]{2,1,0:T(8,128)S(1)} %copy-done.1) | data formatting | bytes 8388608
  191.2 1.6 copy-done
  192.8 2.0 %copy.34 = f32[2,512,1024]{2,1,0:T(8,128)} copy(f32[2,512,1024]{2,1,0:T(8,128)S(1)} %copy-done) | data formatting | bytes 8388608
  (2 shorter events, 0.1 us)
Async XLA Ops:
  177.7 5.8 %copy-start.2 = (bf16[256,1024]{1,0:T(8,128)(2,1)S(1)}, bf16[256,1024]{1,0:T(8,128)(2,1)}, u32[]{:S(2)}) copy-start(bf16[256,1024]{1,0:T(8,128)(2,1)} %get-tuple-element.24) | copy-start | bytes 1572868
  184.2 4.8 %copy-start.1 = (f32[2,1024,512]{2,1,0:T(8,128)S(1)}, f32[2,1024,512]{2,1,0:T(8,128)}, u32[]{:S(2)}) copy-start(f32[2,1024,512]{2,1,0:T(8,128)} %get-tuple-element.27) | copy-start | bytes 12582916
  189.1 3.7 %copy-start = (f32[2,512,1024]{2,1,0:T(8,128)S(1)}, f32[2,512,1024]{2,1,0:T(8,128)}, u32[]{:S(2)}) copy-start(f32[2,512,1024]{2,1,0:T(8,128)} %get-tuple-element.28) | copy-start | bytes 12582916

commit v3 on v1

v3 whole, which is shorter than its diff:
```python
import jax
import jax.numpy as jnp
from jax import lax
from jax.experimental import pallas as pl
from jax.experimental.pallas import tpu as pltpu
from jax.sharding import PartitionSpec as P

F32 = jnp.float32
BF16 = jnp.bfloat16
VMEM = pltpu.VMEM
DMA = pltpu.SemaphoreType.DMA
ANY = pl.BlockSpec(memory_space=pl.ANY)
VM = pl.BlockSpec(memory_space=pltpu.VMEM)


def position():
    me = lax.axis_index("ep")
    return me, me // 4, (me // 2) % 2, me % 2


def mirror(z, v):
    return v + (z // 2) * (3 - 2 * v)


def near_first(z, k):
    q = mirror(z, z)
    return mirror(z, (q, 1 - q, 2, 3)[k])


def dot_nt(a, b):
    return lax.dot_general(a, b, (((1,), (1,)), ((), ())), preferred_element_type=F32)


def dot_tn(a, b):
    return lax.dot_general(a, b, (((0,), (0,)), ((), ())), preferred_element_type=F32)


def one_hot(slot, cap):
    return slot == lax.broadcasted_iota(jnp.int32, (cap, slot.shape[1]), 0).astype(F32)


def step_kernel(gy, idx_t, slot_t, gate_t, counts, yr_hbm, hg_hbm, hu_hbm, wd_hbm, wg_hbm, wu_hbm, x_hbm, gx, gg, gwd_hbm, gwg_hbm, gwu_hbm,
                tok, meta, meta_out, hbuf, wd, wg, wu, xs, yr, d_ref, a_ref, dh1, dh3, acc, r_own, r_send, r_recv, tot, z_in, y_send, y_in, f_send, f_recv, og, ou,
                w_sem, h_sem, x_sem, g_sem, st_sem, acc_sem, send, recv, m_send, m_recv, rs, rr, ys, yrs, zs_sem, zr_sem, fs, fr):
    me, z, y, c = position()
    n_loc, n_rows, ffn = dh1.shape
    cap = n_rows // 16
    half = r_own.shape[3]
    n_exp = counts.shape[1]
    sib = me + 1 - 2 * c
    ynb = me + 2 - 4 * y
    m = z // 2
    q = mirror(z, z)
    way = 1 - 2 * m
    end = q == 0
    mid = q == 1
    up = (me + 4 * way + 16) % 16
    down = (me - 4 * way + 16) % 16

    order = ((0, 0), (1, 0), (0, 1), (2, 0), (1, 1), (3, 0), (2, 1), (3, 1))

    def chip_of(t):
        k, other = order[t]
        return near_first(z, k), y + other * (1 - 2 * y)

    def rows_of(chip):
        return pl.ds(pl.multiple_of(chip * 2 * cap, 2 * cap), 2 * cap)

    def h_loads(t):
        d, yy = chip_of(t)
        rows = rows_of(d * 2 + yy)
        return [pltpu.make_async_copy(src.at[:, rows, :], hbuf.at[t % 2, i], h_sem.at[t % 2, i]) for i, src in enumerate((hg_hbm, hu_hbm))]

    w_loads = [pltpu.make_async_copy(src, dst, w_sem.at[i]) for i, (src, dst) in enumerate(((wd_hbm, wd), (wg_hbm, wg), (wu_hbm, wu)))]
    for cp in h_loads(0) + w_loads:
        cp.start()

    def yr_load(i):
        return pltpu.make_async_copy(yr_hbm.at[pl.ds(pl.multiple_of(i * 256, 256), 256), :], yr.at[i % 2], g_sem.at[i % 2])

    yr_load(0).start()

    barrier = pltpu.get_barrier_semaphore()
    for k in range(1, 16):
        pl.semaphore_signal(barrier, inc=1, device_id={"ep": (me + k) % 16})

    idx, slots, gates = idx_t[...], slot_t[...], gate_t[...]
    for e in range(n_exp):
        hit = idx == e
        slot = jnp.max(jnp.where(hit, slots, -1), axis=0, keepdims=True)
        slot = jnp.where(slot < counts[0, e], slot, -1)
        meta_out[e // 4, e % 4] = slot.astype(F32)
        meta_out[e // 4, 4 + e % 4] = jnp.sum(jnp.where(hit, gates, 0.0), axis=0, keepdims=True)
    pl.semaphore_wait(barrier, 15)

    def put(src, slot, link, to):
        return pltpu.make_async_remote_copy(src_ref=src, dst_ref=tok.at[slot], send_sem=send.at[slot, link], recv_sem=recv.at[slot], device_id={"ep": to})

    def arrive(slot):
        put(tok.at[slot], slot, 0, me).wait_recv()

    def meta_copy(k):
        to = (me + k) % 16
        return pltpu.make_async_remote_copy(src_ref=meta_out.at[to // 2], dst_ref=meta.at[me], send_sem=m_send.at[k], recv_sem=m_recv.at[me], device_id={"ep": to})

    own = [(put(gy, me, 0, up), None), (put(gy, me, 1, down), mid), (put(gy, me, 2, ynb), None), (put(gy, me, 3, sib), None)]
    for cp, cond in own:
        cp.start() if cond is None else pl.when(cond)(cp.start)
    for k in range(1, 16):
        meta_copy(k).start()
    tok[me] = gy[...]
    meta[me] = meta_out[me // 2]
    acc[...] = jnp.zeros_like(acc)

    gg[...] = jnp.zeros_like(gg)

    def gate_block(i, _):
        yr_load(i).wait()

        @pl.when(i < 7)
        def _():
            yr_load(i + 1).start()

        base = pl.multiple_of((i // 4) * 128, 128)
        prod = dot_nt(yr[i % 2], gy[pl.ds(base, 128), :]).reshape(32, 8, 128)
        t = lax.broadcasted_iota(jnp.int32, prod.shape, 0) + (i % 4) * 32
        mine = t == lax.broadcasted_iota(jnp.int32, prod.shape, 2)
        gg[:, pl.ds(base, 128)] += jnp.sum(jnp.where(mine, prod, 0.0), axis=0)
        return 0

    lax.fori_loop(0, 8, gate_block, 0)
    for k in range(1, 16):
        src = (me + k) % 16
        pltpu.make_async_remote_copy(src_ref=meta_out.at[0], dst_ref=meta.at[src], send_sem=m_send.at[k], recv_sem=m_recv.at[src], device_id={"ep": src}).wait_recv()
    for cp in w_loads:
        cp.wait()

    def token_slot(k, ys_, cs):
        return near_first(z, k) * 4 + ys_ * 2 + cs

    def relay_to(k):
        zs = near_first(z, k)
        away = jnp.where(zs < z, 1, -1)
        nz = z + away
        return (me + 4 * away + 16) % 16, (nz >= 0) & (nz <= 3)

    def relay(k, cond=None):
        slot = token_slot(k, y, c)
        to, inside = relay_to(k)

        def body():
            arrive(slot)
            pl.when(inside)(put(tok.at[slot], slot, 0, to).start)
            put(tok.at[slot], slot, 2, ynb).start()
            put(tok.at[slot], slot, 3, sib).start()

        body() if cond is None else pl.when(cond)(body)

    def y_arrival(k):
        slot = token_slot(k, 1 - y, c)
        arrive(slot)
        put(tok.at[slot], slot, 3, sib).start()

    def z_slot(w, d, k, leftward, to_z):
        return jnp.where(leftward & (d == to_z), 12 + k, w)

    def z_copy(w, d, k, step):
        dst = z_slot(w, d, k, step < 0, z + step)
        return pltpu.make_async_remote_copy(src_ref=tot.at[w], dst_ref=z_in.at[dst], send_sem=zs_sem.at[w], recv_sem=zr_sem.at[dst], device_id={"ep": (me + 4 * step + 16) % 16})

    def z_add(w, d, k, step):
        src = z_slot(w, d, k, step < 0, z)
        pltpu.make_async_remote_copy(src_ref=tot.at[w], dst_ref=z_in.at[src], send_sem=zs_sem.at[w], recv_sem=zr_sem.at[src], device_id={"ep": me}).wait_recv()
        tot[w] = tot[w] + z_in[src]

    def y_copy(i, src):
        return pltpu.make_async_remote_copy(src_ref=src, dst_ref=y_in.at[i], send_sem=ys.at[i], recv_sem=yrs.at[i], device_id={"ep": ynb})

    def y_add(w, i):
        y_copy(i, y_send.at[0]).wait_recv()
        tot[w] = tot[w] + y_in[i]

    def unit0(dq, other):
        d = mirror(z, dq)
        yy = y + other * (1 - 2 * y)
        return d * 2 + yy, d, yy

    def unit1(dq):
        d = mirror(z, dq)
        return 8 + d, d, 2

    def start_up(unit):
        z_copy(*unit, way).start()

    def pass_up(unit):
        z_add(*unit, way)
        z_copy(*unit, way).start()

    def pass_down(unit):
        z_add(*unit, -way)
        z_copy(*unit, -way).start()

    def swap(chip, slot):
        return pltpu.make_async_remote_copy(src_ref=r_send.at[slot], dst_ref=r_recv.at[chip], send_sem=rs.at[chip], recv_sem=rr.at[chip], device_id={"ep": sib})

    def make(t, slot):
        d, yy = chip_of(t)
        chip = d * 2 + yy
        rows = rows_of(chip)
        for cp in h_loads(t):
            cp.wait()
        if t < 7:
            for cp in h_loads(t + 1):
                cp.start()

        def per_expert(e, _):
            for h in range(2):
                s = chip * 2 + h
                hot = one_hot(meta[s, c * 2 + e], cap)
                gate = jnp.sum(jnp.where(hot, meta[s, 4 + c * 2 + e], 0.0), axis=1, keepdims=True)
                picked = jnp.dot(jnp.where(hot, 1.0, 0.0).astype(BF16), tok[s], preferred_element_type=F32)
                d_ref[h * cap:(h + 1) * cap, :] = (picked * gate).astype(BF16)
            g = dot_nt(d_ref[...], wd[e]).astype(BF16).astype(F32)
            h1 = hbuf[t % 2, 0, e].astype(F32)
            h3 = hbuf[t % 2, 1, e].astype(F32)
            sig = jax.nn.sigmoid(h1)
            act = h1 * sig
            a_ref[...] = (act * h3).astype(BF16)
            dh1[e, rows, :] = (g * h3 * sig * (1.0 + h1 * (1.0 - sig))).astype(BF16)
            dh3[e, rows, :] = (g * act).astype(BF16)
            for part, dest in ((1 - c, r_send), (c, r_own)):
                cols = pl.ds(pl.multiple_of(part * half, half), half)
                r = dot_nt(dh1[e, rows, :], wg[e, cols, :]) + dot_nt(dh3[e, rows, :], wu[e, cols, :])
                dest[slot, e] = r.astype(BF16)
            acc[e] += dot_tn(a_ref[...], d_ref[...])
            return 0

        lax.fori_loop(0, n_loc, per_expert, 0)
        swap(chip, slot).start()

    def combine(t, slot):
        d, yy = chip_of(t)
        chip = d * 2 + yy
        cp = swap(chip, slot)
        cp.wait_recv()
        for h in range(2):
            s = chip * 2 + h
            lanes = pl.ds(h * cap, cap)
            ids = (c * 2, c * 2 + 1, 2 - c * 2, 3 - c * 2)
            pick = jnp.concatenate([jnp.where(one_hot(meta[s, i], cap), 1.0, 0.0).astype(BF16) for i in ids], axis=0)
            vals = jnp.concatenate([r_own[slot, 0, lanes, :], r_own[slot, 1, lanes, :], r_recv[chip, 0, lanes, :], r_recv[chip, 1, lanes, :]], axis=0)
            part = dot_tn(pick, vals)
            if h == 0:
                tot[d * 2 + yy] = part
            elif order[t][1] == 0:
                tot[8 + d] = part
            else:
                y_send[d] = part
        cp.wait_send()

    def y_start(dq):
        d = mirror(z, dq)
        y_copy(d, y_send.at[d]).start()

    arrive(token_slot(0, y, 1 - c))
    make(0, 0)
    combine(0, 0)
    for phase in range(1, 5):
        if phase == 1:
            relay(1)
            relay(2, mid)
        elif phase == 2:
            relay(2, end)
            relay(3, mid)
        elif phase == 3:
            relay(3, end)
        if phase < 4:
            arrive(token_slot(phase, y, 1 - c))
            make(2 * phase - 1, 0)
        y_arrival(phase - 1)
        if phase < 4:
            combine(2 * phase - 1, 0)
            pl.when(end)(lambda phase=phase: start_up(unit0(phase, 0)))
        arrive(token_slot(phase - 1, 1 - y, 1 - c))
        make(2 * phase if phase < 4 else 7, 1)
        combine(2 * phase if phase < 4 else 7, 1)
        if phase == 3:
            @pl.when(end)
            def _():
                start_up(unit0(2, 1))
                y_start(2)

            @pl.when(mid)
            def _():
                y_start(0)
                pass_up(unit0(2, 0))
        if phase == 4:
            y_start(3)

            @pl.when(end)
            def _():
                start_up(unit0(3, 1))
                y_start(1)
                y_start(0)

            @pl.when(mid)
            def _():
                y_start(2)
                y_start(1)
                pass_up(unit0(3, 0))

    width = xs.shape[2]

    def x_load(i):
        e, t = i // 4, i % 4
        return pltpu.make_async_copy(x_hbm.at[e, :, pl.ds(pl.multiple_of(t * width, width), width)], xs.at[i % 2], x_sem.at[i % 2])

    def w_out(i):
        e, t = i // 4, i % 4
        rows = pl.ds(pl.multiple_of(t * width, width), width)
        return (pltpu.make_async_copy(og.at[i % 2], gwg_hbm.at[e, rows, :], st_sem.at[i % 2, 0]),
                pltpu.make_async_copy(ou.at[i % 2], gwu_hbm.at[e, rows, :], st_sem.at[i % 2, 1]))

    def through_y(dq, go):
        unit = unit1(dq)
        y_add(unit[0], unit[1])
        go(unit)

    mid_events = (
        lambda: pass_up(unit0(2, 1)),
        lambda: pass_down(unit0(0, 0)),
        lambda: pass_up(unit0(3, 1)),
        lambda: through_y(3, pass_up),
        lambda: pass_down(unit0(0, 1)),
        lambda: through_y(2, pass_up),
        lambda: through_y(0, pass_down),
    )
    end_events = (
        None,
        lambda: through_y(3, start_up),
        lambda: through_y(2, start_up),
        lambda: start_up(unit0(1, 1)),
        lambda: through_y(1, start_up),
    )
    x_load(0).start()
    acc_out = pltpu.make_async_copy(acc, gwd_hbm, acc_sem.at[0])
    acc_out.start()

    def weights(i, _):
        x_load(i).wait()

        @pl.when(i < 7)
        def _():
            x_load(i + 1).start()

        @pl.when(i >= 2)
        def _():
            for cp in w_out(i - 2):
                cp.wait()

        e = i // 4
        og[i % 2] = dot_tn(xs[i % 2], dh1[e])
        ou[i % 2] = dot_tn(xs[i % 2], dh3[e])
        for cp in w_out(i):
            cp.start()
        for n, event in enumerate(mid_events):
            pl.when(mid & (i == n))(event)
        for n, event in enumerate(end_events):
            if event is not None:
                pl.when(end & (i == n))(event)
        return 0

    lax.fori_loop(0, 8, weights, 0)

    def finish(unit):
        z_add(*unit, -way)
        pl.when(mid)(lambda: z_add(*unit, way))

    own0, cross0, own1 = unit0(q, 0), unit0(q, 1), unit1(q)

    def last():
        return pltpu.make_async_remote_copy(src_ref=f_send, dst_ref=f_recv, send_sem=fs.at[0], recv_sem=fr.at[0], device_id={"ep": sib})

    def deliver(w, h):
        @pl.when(c == h)
        def _():
            gx[:, h * half:(h + 1) * half] = tot[w].astype(BF16)

        @pl.when(c != h)
        def _():
            f_send[...] = tot[w].astype(BF16)
            last().start()

    finish(own0)
    finish(cross0)
    y_copy(4, tot.at[cross0[0]]).start()
    y_add(own1[0], own1[1])
    finish(own1)
    deliver(own1[0], 1)
    y_add(own0[0], 4)
    deliver(own0[0], 0)
    last().wait()
    for h in range(2):
        @pl.when(c == h)
        def _():
            gx[:, (1 - h) * half:(2 - h) * half] = f_recv[...]

    for cp, cond in own:
        cp.wait_send() if cond is None else pl.when(cond)(cp.wait_send)
    for k in range(1, 4):
        slot = token_slot(k, y, c)
        pl.when(relay_to(k)[1])(put(tok.at[slot], slot, 0, me).wait_send)
        put(tok.at[slot], slot, 2, ynb).wait_send()
        put(tok.at[slot], slot, 3, sib).wait_send()
    for k in range(4):
        slot = token_slot(k, 1 - y, c)
        put(tok.at[slot], slot, 3, sib).wait_send()
    for k in range(1, 16):
        meta_copy(k).wait_send()
    for d in range(4):
        y_copy(d, y_send.at[d]).wait_send()
    y_copy(4, tot.at[cross0[0]]).wait_send()

    def z_drain(w, d):
        pl.when(d != z)(pltpu.make_async_remote_copy(src_ref=tot.at[w], dst_ref=z_in.at[w], send_sem=zs_sem.at[w], recv_sem=zr_sem.at[w], device_id={"ep": me}).wait_send)

    for w in range(8):
        z_drain(w, w // 2)
    for d in range(4):
        z_drain(8 + d, d)
    for i in (6, 7):
        for cp in w_out(i):
            cp.wait()
    acc_out.wait()


def solution(mesh):
    rows_spec = P(("dp", "ep"), None)
    cube_spec = P(("dp", "ep"), None, None)
    weight_spec = P("ep", None, None)

    def local_step(grad_y, gate_vals, topk_idx, slot_ids, pair_counts, y_routed, x_disp, h_gate, h_up, w_gate, w_up, w_down):
        n_loc, n_rows, ffn = h_gate.shape
        tok, dim = grad_y.shape
        top_k = topk_idx.shape[1]
        half = dim // 2
        cap = n_rows // 16
        shape = jax.ShapeDtypeStruct
        grad_x, grad_gate, grad_wdown, grad_wgate, grad_wup = pl.pallas_call(
            step_kernel,
            out_shape=(shape((tok, dim), BF16), shape((top_k, tok), F32), shape((n_loc, ffn, dim), F32), shape((n_loc, dim, ffn), F32), shape((n_loc, dim, ffn), F32)),
            in_specs=[VM, VM, VM, VM, pl.BlockSpec(memory_space=pltpu.SMEM)] + [ANY] * 7,
            out_specs=(VM, VM, ANY, ANY, ANY),
            scratch_shapes=[
                VMEM((16, tok, dim), BF16), VMEM((16, 8, 1, tok), F32), VMEM((8, 8, 1, tok), F32),
                VMEM((2, 2, n_loc, 2 * cap, ffn), BF16),
                VMEM((n_loc, ffn, dim), BF16), VMEM((n_loc, dim, ffn), BF16), VMEM((n_loc, dim, ffn), BF16),
                VMEM((2, n_rows, 256), BF16), VMEM((2, 256, dim), BF16),
                VMEM((2 * cap, dim), BF16), VMEM((2 * cap, ffn), BF16),
                VMEM((n_loc, n_rows, ffn), BF16), VMEM((n_loc, n_rows, ffn), BF16), VMEM((n_loc, ffn, dim), F32),
                VMEM((2, n_loc, 2 * cap, half), BF16), VMEM((2, n_loc, 2 * cap, half), BF16), VMEM((8, n_loc, 2 * cap, half), BF16),
                VMEM((12, tok, half), F32), VMEM((15, tok, half), F32), VMEM((4, tok, half), F32), VMEM((5, tok, half), F32),
                VMEM((tok, half), BF16), VMEM((tok, half), BF16),
                VMEM((2, 256, ffn), F32), VMEM((2, 256, ffn), F32),
                DMA((3,)), DMA((2, 2)), DMA((2,)), DMA((2,)), DMA((2, 2)), DMA((1,)),
                DMA((16, 4)), DMA((16,)), DMA((16,)), DMA((16,)), DMA((8,)), DMA((8,)), DMA((5,)), DMA((5,)), DMA((12,)), DMA((15,)), DMA((1,)), DMA((1,)),
            ],
            compiler_params=pltpu.CompilerParams(collective_id=1, has_side_effects=True, vmem_limit_bytes=67043328),
            name="step",
        )(grad_y, topk_idx.T, slot_ids.T, gate_vals.T, pair_counts, y_routed.reshape(tok * top_k, dim), h_gate, h_up, w_down, w_gate, w_up, x_disp)
        return grad_x, grad_gate.T, grad_wgate, grad_wup, grad_wdown

    return jax.shard_map(local_step, mesh=mesh, in_specs=(rows_spec, rows_spec, rows_spec, rows_spec, rows_spec, cube_spec, cube_spec, cube_spec, cube_spec, weight_spec, weight_spec, weight_spec), out_specs=(rows_spec, rows_spec, cube_spec, cube_spec, cube_spec), check_vma=False)
```

time: 333 us -> 161 us (0.48)
  waiting for transfers between devices: 184 us -> 0 us
  Pallas kernels: 0 us -> 146 us
  matrix products: 95.5 us -> 0 us
  between operations: 14.1 us -> 0.65 us
  other arithmetic: 8.28 us -> 0 us
  local copies, waits for them, and re-layouts: 21.3 us -> 13.7 us
  starting transfers between devices: 6.54 us -> 0 us
    pallas_call x0 -> x1, Pallas kernels: none -> 146 us  [local_step(): pl.pallas_call(step_kernel, out_shape=(shape((tok, dim), BF16), shape((to...]
    reduce_scatter x1 -> x0, waiting for transfers between devices: 120 us -> none  [local_step(): lax.psum_scatter(part.reshape(n_dev * tok, model_dim), 'ep', scatter_dime...]
    dot_general x9 -> x0, matrix products: 95.5 us -> none  [the longest x1 14.1 us: local_step(): jnp.einsum('erd,efd->erf', grad_rows, w_down, preferred_element_type=F32)]
    all_gather x1 -> x0, waiting for transfers between devices: 59.6 us -> none  [local_step(): all_y = lax.all_gather(grad_y, 'ep')]
    convert_element_type x1 -> x0, local copies, waits for them, and re-layouts: 8.18 us -> none  [local_step(): (rows * jnp.transpose(gate_rows, (1, 0, 2))[..., None]).astype(BF16)]
    all_to_all x1 -> x0, starting transfers between devices: 6.47 us -> none  [local_step(): meta = lax.all_to_all(meta, 'ep', 0, 0)]
    all_to_all x1 -> x0, waiting for transfers between devices: 4.28 us -> none  [local_step(): meta = lax.all_to_all(meta, 'ep', 0, 0)]
    unnamed x15 -> x9, local copies, waits for them, and re-layouts: 12.3 us -> 13.7 us
  transfers between devices with their start and end apart: 3 -> 0, of which waited for: 3 -> 0; matrix products, arithmetic and copies ran while one was open for 18% -> 0% of each run, Pallas kernels for 0% -> 0%
where the time goes in v3:
time: 161 us; the launch traced here: 160 us
  Pallas kernels  146 us (91%)
  local copies, waits for them, and re-layouts  13.7 us (9%)
    pallas_call x1, Pallas kernels, local_step(): pl.pallas_call(step_kernel, out_shape=(shape((tok, dim), BF16), shape((to...  146 us
    unnamed x9, local copies, waits for them, and re-layouts  13.7 us

profile of v3, /device:TPU:19, one launch (start us, length us, event | category | flops | bytes accessed | tf_op | source)
XLA Modules:
  0.0 160.1 jit_solution(10864280670348304590)
XLA Ops:
  0.6 145.7 %step.1 = (bf16[256,1024]{1,0:T(8,128)(2,1)}, f32[8,256]{1,0:T(8,128)}, f32[2,512,1024]{2,1,0:T(8,128)}, f32[2,1024,512]{2,1,0:T(8,128)}, f32[2,1024,512]{2,1,0:T(8,128)}) custom-call(bf16[256,1024]{1,0:T(8,128)(2,1)} %gy.1, s32[8,256]{1,0:T(8,128)} %bitcast.6, s32[8,256]{1,0:T(8,128)} %bitcast.7, f32[8,256]{1,0:T(8,128)} %bitcast.8, s32[1,32]{1,0:T(1,128)} %counts.1, ...), custom_call_target="tpu_custom_call" | custom-call | tf_op jit(solution)/shard_map/step/pallas_call | solution.py:449
  146.4 1.9 %copy.22 = bf16[256,1024]{1,0:T(8,128)(2,1)} copy(bf16[256,1024]{1,0:T(8,128)(2,1)} %get-tuple-element.20) | data formatting | bytes 1048576
  148.2 1.3 copy.23
  149.5 0.0 copy-start.1
  149.5 4.8 %copy.24 = f32[2,1024,512]{2,1,0:T(8,128)} copy(f32[2,1024,512]{2,1,0:T(8,128)} %get-tuple-element.22) | data formatting | bytes 8388608
  154.4 0.0 copy-done.1
  154.4 0.0 copy-start
  154.4 2.1 %copy.25 = f32[2,1024,512]{2,1,0:T(8,128)} copy(f32[2,1024,512]{2,1,0:T(8,128)S(1)} %copy-done.1) | data formatting | bytes 8388608
  156.5 1.6 copy-done
  158.1 2.0 %copy.26 = f32[2,512,1024]{2,1,0:T(8,128)} copy(f32[2,512,1024]{2,1,0:T(8,128)S(1)} %copy-done) | data formatting | bytes 8388608
Async XLA Ops:
  149.5 4.8 %copy-start.1 = (f32[2,1024,512]{2,1,0:T(8,128)S(1)}, f32[2,1024,512]{2,1,0:T(8,128)}, u32[]{:S(2)}) copy-start(f32[2,1024,512]{2,1,0:T(8,128)} %get-tuple-element.23) | copy-start | bytes 12582916
  154.4 3.7 %copy-start = (f32[2,512,1024]{2,1,0:T(8,128)S(1)}, f32[2,512,1024]{2,1,0:T(8,128)}, u32[]{:S(2)}) copy-start(f32[2,512,1024]{2,1,0:T(8,128)} %get-tuple-element.24) | copy-start | bytes 12582916

commit v4 on v3

--- a/solution.py
+++ b/solution.py
@@ -432,6 +432,40 @@
         for cp in w_out(i):
             cp.wait()
     acc_out.wait()
+
+
+def deliver_kernel(*refs):
+    n = (len(refs) - 2) // 3
+    src, dst, buf, (in_sem, out_sem) = refs[:n], refs[n:2 * n], refs[2 * n:3 * n], refs[3 * n:]
+    pieces = []
+    for s, d, b in zip(src, dst, buf):
+        rows = s.shape[-2]
+        parts = 2 if len(s.shape) == 3 else 1
+        for lead in ([(e,) for e in range(s.shape[0])] if len(s.shape) == 3 else [()]):
+            for k in range(parts):
+                at = lead + (pl.ds(k * rows // parts, rows // parts),)
+                i = len(pieces)
+                pieces.append((pltpu.make_async_copy(s.at[at], b.at[at], in_sem.at[i]), pltpu.make_async_copy(b.at[at], d.at[at], out_sem.at[i])))
+    for read, _ in pieces:
+        read.start()
+    for read, write in pieces:
+        read.wait()
+        write.start()
+    for _, write in pieces:
+        write.wait()
+
+
+def deliver(arrays):
+    n = 2 + 4 * (len(arrays) - 2)
+    return pl.pallas_call(
+        deliver_kernel,
+        out_shape=tuple(jax.ShapeDtypeStruct(a.shape, a.dtype) for a in arrays),
+        in_specs=[ANY] * len(arrays),
+        out_specs=(ANY,) * len(arrays),
+        scratch_shapes=[VMEM(a.shape, a.dtype) for a in arrays] + [DMA((n,)), DMA((n,))],
+        compiler_params=pltpu.CompilerParams(vmem_limit_bytes=67043328),
+        name="deliver",
+    )(*arrays)
 
 
 def solution(mesh):
@@ -468,6 +502,7 @@
             compiler_params=pltpu.CompilerParams(collective_id=1, has_side_effects=True, vmem_limit_bytes=67043328),
             name="step",
         )(grad_y, topk_idx.T, slot_ids.T, gate_vals.T, pair_counts, y_routed.reshape(tok * top_k, dim), h_gate, h_up, w_down, w_gate, w_up, x_disp)
+        grad_wgate, grad_wup, grad_wdown, grad_x, grad_gate = deliver((grad_wgate, grad_wup, grad_wdown, grad_x, grad_gate))
         return grad_x, grad_gate.T, grad_wgate, grad_wup, grad_wdown
 
     return jax.shard_map(local_step, mesh=mesh, in_specs=(rows_spec, rows_spec, rows_spec, rows_spec, rows_spec, cube_spec, cube_spec, cube_spec, cube_spec, weight_spec, weight_spec, weight_spec), out_specs=(rows_spec, rows_spec, cube_spec, cube_spec, cube_spec), check_vma=False)

time: 161 us -> 156 us (0.969)
  local copies, waits for them, and re-layouts: 13.7 us -> 0 us
  Pallas kernels: 146 us -> 155 us
    unnamed x9 -> x0, local copies, waits for them, and re-layouts: 13.7 us -> none
    pallas_call x0 -> x1, Pallas kernels: none -> 9.41 us  [deliver(): pl.pallas_call(deliver_kernel, out_shape=tuple((jax.ShapeDtypeStruct(a.sh...]
where the time goes in v4:
time: 156 us
  Pallas kernels  155 us (99%)
    pallas_call x1, Pallas kernels, local_step(): pl.pallas_call(step_kernel, out_shape=(shape((tok, dim), BF16), shape((to...  146 us
    pallas_call x1, Pallas kernels, deliver(): pl.pallas_call(deliver_kernel, out_shape=tuple((jax.ShapeDtypeStruct(a.sh...  9.41 us

profile of v4, /device:TPU:19, one launch (start us, length us, event | category | flops | bytes accessed | tf_op | source)
XLA Modules:
  0.0 156.0 jit_solution(18179701389616440004)
XLA Ops:
  0.6 145.7 %step.1 = (bf16[256,1024]{1,0:T(8,128)(2,1)}, f32[8,256]{1,0:T(8,128)}, f32[2,512,1024]{2,1,0:T(8,128)}, f32[2,1024,512]{2,1,0:T(8,128)}, f32[2,1024,512]{2,1,0:T(8,128)}) custom-call(bf16[256,1024]{1,0:T(8,128)(2,1)} %gy.1, s32[8,256]{1,0:T(8,128)} %bitcast.6, s32[8,256]{1,0:T(8,128)} %bitcast.7, f32[8,256]{1,0:T(8,128)} %bitcast.8, s32[1,32]{1,0:T(1,128)} %counts.1, ...), custom_call_target="tpu_custom_call" | custom-call | tf_op jit(solution)/shard_map/step/pallas_call | solution.py:483
  146.4 9.4 %deliver.1 = (f32[2,1024,512]{2,1,0:T(8,128)}, f32[2,1024,512]{2,1,0:T(8,128)}, f32[2,512,1024]{2,1,0:T(8,128)}, bf16[256,1024]{1,0:T(8,128)(2,1)}, f32[8,256]{1,0:T(8,128)}) custom-call(f32[2,1024,512]{2,1,0:T(8,128)} %get-tuple-element.15.refs_0_, f32[2,1024,512]{2,1,0:T(8,128)} %get-tuple-element.16.refs_1_, f32[2,512,1024]{2,1,0:T(8,128)} %get-tuple-element.17.refs_2_, ...), custom_call_target="tpu_custom_call" | custom-call | tf_op jit(solution)/shard_map/deliver/pallas_call | solution.py:460

commit v5 on v4

v5 whole, which is shorter than its diff:
```python
import jax
import jax.numpy as jnp
from jax import lax
from jax.experimental import pallas as pl
from jax.experimental.pallas import tpu as pltpu
from jax.sharding import PartitionSpec as P

F32 = jnp.float32
BF16 = jnp.bfloat16
VMEM = pltpu.VMEM
DMA = pltpu.SemaphoreType.DMA
Z0, Z1, Z2, Z3 = range(4)
OWN, OTHER = CORE0, CORE1 = LO, HI = CORES = HALVES = range(2)
ONWARD, DOWN, CROSS, CORE = range(4)
NZ, GROUP = 4, 16
PEERS = range(1, GROUP)
ANY = pl.BlockSpec(memory_space=pl.ANY)
VM = pl.BlockSpec(memory_space=pltpu.VMEM)


def position():
    me = lax.axis_index("ep")
    return me, me // 4, (me // 2) % 2, me % 2


def mirror(z, v):
    return v + (z // 2) * (3 - 2 * v)


def dot_nt(a, b):
    return lax.dot_general(a, b, (((1,), (1,)), ((), ())), preferred_element_type=F32)


def dot_tn(a, b):
    return lax.dot_general(a, b, (((0,), (0,)), ((), ())), preferred_element_type=F32)


def one_hot(slot, cap):
    return slot == lax.broadcasted_iota(jnp.int32, (cap, slot.shape[1]), 0).astype(F32)


def step_kernel(gy, idx_t, slot_t, gate_t, counts, yr_hbm, hg_hbm, hu_hbm, wd_hbm, wg_hbm, wu_hbm, x_hbm, gx, gg, gwd_hbm, gwg_hbm, gwu_hbm,
                tok, meta, meta_out, hbuf, wd, wg, wu, xs, yr, d_ref, a_ref, dh1, dh3, acc, r_own, r_send, r_recv, tot, z_in, y_in, f_send, f_recv, og, ou,
                w_sem, h_sem, x_sem, g_sem, st_sem, acc_sem, send, recv, m_send, m_recv, rs, rr, ys, yrs, zs_sem, zr_sem, fs, fr):
    me, z, y, c = position()
    n_loc, n_rows, ffn = dh1.shape
    cap = n_rows // 16
    half = r_own.shape[3]
    n_exp = counts.shape[1]
    sib = me + 1 - 2 * c
    ynb = me + 2 - 4 * y
    m = z // 2
    q = mirror(z, z)
    way = 1 - 2 * m
    end = q == 0
    mid = q == 1
    up = (me + 4 * way + GROUP) % GROUP
    down = (me - 4 * way + GROUP) % GROUP

    order = (((Z0, OWN), (Z1, OWN)), ((Z0, OTHER), (Z0, OWN)), ((Z1, OWN), (Z2, OWN)), ((Z1, OTHER), (Z1, OTHER)), ((Z2, OWN), (Z0, OTHER)), ((Z2, OTHER), (Z3, OWN)), ((Z3, OWN), (Z2, OTHER)), ((Z3, OTHER), (Z3, OTHER)))

    def chip_of(t):
        (d_end, o_end), (d_mid, o_mid) = order[t]
        other = o_end + q * (o_mid - o_end)
        return mirror(z, d_end + q * (d_mid - d_end)), y + other * (1 - 2 * y)

    def rows_of(chip):
        return pl.ds(pl.multiple_of(chip * 2 * cap, 2 * cap), 2 * cap)

    def h_loads(t):
        d, yy = chip_of(t)
        rows = rows_of(d * 2 + yy)
        return [pltpu.make_async_copy(src.at[:, rows, :], hbuf.at[t % 2, i], h_sem.at[t % 2, i]) for i, src in enumerate((hg_hbm, hu_hbm))]

    w_loads = [pltpu.make_async_copy(src, dst, w_sem.at[i]) for i, (src, dst) in enumerate(((wd_hbm, wd), (wg_hbm, wg), (wu_hbm, wu)))]
    for cp in h_loads(0) + w_loads:
        cp.start()

    def yr_load(i):
        return pltpu.make_async_copy(yr_hbm.at[pl.ds(pl.multiple_of(i * 256, 256), 256), :], yr.at[i % 2], g_sem.at[i % 2])

    yr_load(0).start()

    barrier = pltpu.get_barrier_semaphore()
    for k in PEERS:
        pl.semaphore_signal(barrier, inc=1, device_id={"ep": (me + k) % GROUP})

    idx, slots, gates = idx_t[...], slot_t[...], gate_t[...]
    for e in range(n_exp):
        hit = idx == e
        slot = jnp.max(jnp.where(hit, slots, -1), axis=0, keepdims=True)
        slot = jnp.where(slot < counts[0, e], slot, -1)
        meta_out[e // 4, e % 4] = slot.astype(F32)
        meta_out[e // 4, 4 + e % 4] = jnp.sum(jnp.where(hit, gates, 0.0), axis=0, keepdims=True)
    pl.semaphore_wait(barrier, 15)

    part_rows = gy.shape[0] // 2

    def part(p):
        return pl.ds(p * part_rows, part_rows)

    def put(slot, link, to, p, src=None):
        src = tok.at[slot, part(p)] if src is None else src
        return pltpu.make_async_remote_copy(src_ref=src, dst_ref=tok.at[slot, part(p)], send_sem=send.at[slot, link, p], recv_sem=recv.at[slot, p], device_id={"ep": to})

    def arrive(slot, p):
        put(slot, 0, me, p).wait_recv()

    def meta_copy(k):
        to = (me + k) % GROUP
        return pltpu.make_async_remote_copy(src_ref=meta_out.at[to // 2], dst_ref=meta.at[me], send_sem=m_send.at[k], recv_sem=m_recv.at[me], device_id={"ep": to})

    own = [(put(me, link, to, p, gy.at[part(p)]), cond) for p in HALVES for link, to, cond in ((ONWARD, up, None), (DOWN, down, mid), (CROSS, ynb, None), (CORE, sib, None))]
    for cp, cond in own:
        cp.start() if cond is None else pl.when(cond)(cp.start)
    for k in PEERS:
        meta_copy(k).start()
    tok[me] = gy[...]
    meta[me] = meta_out[me // 2]
    acc[...] = jnp.zeros_like(acc)

    gg[...] = jnp.zeros_like(gg)

    def gate_block(i, _):
        yr_load(i).wait()

        @pl.when(i < 7)
        def _():
            yr_load(i + 1).start()

        base = pl.multiple_of((i // 4) * 128, 128)
        prod = dot_nt(yr[i % 2], gy[pl.ds(base, 128), :]).reshape(32, 8, 128)
        t = lax.broadcasted_iota(jnp.int32, prod.shape, 0) + (i % 4) * 32
        mine = t == lax.broadcasted_iota(jnp.int32, prod.shape, 2)
        gg[:, pl.ds(base, 128)] += jnp.sum(jnp.where(mine, prod, 0.0), axis=0)
        return 0

    lax.fori_loop(0, 8, gate_block, 0)
    for k in PEERS:
        src = (me + k) % GROUP
        pltpu.make_async_remote_copy(src_ref=meta_out.at[0], dst_ref=meta.at[src], send_sem=m_send.at[k], recv_sem=m_recv.at[src], device_id={"ep": src}).wait_recv()
    for cp in w_loads:
        cp.wait()

    def home(d, other, h):
        return mirror(z, d) * 4 + (y + other * (1 - 2 * y)) * 2 + h

    def relay(d, other, p, links):
        slot = home(d, other, c)
        arrive(slot, p)
        for link in links:
            put(slot, link, ynb if link == CROSS else sib if link == CORE else up if d == Z0 else down, p).start()

    def y_arrival(d, p, onward=False):
        slot = home(d, 1, c)
        arrive(slot, p)
        if onward:
            put(slot, ONWARD, up, p).start()
        put(slot, CORE, sib, p).start()

    def z_base(d, other, h):
        return mirror(z, d) * 2 + h if other == 0 else 7 + mirror(z, d)

    def z_slot(d, other, h, leftward, to_z):
        return jnp.where(leftward & (mirror(z, d) == to_z), 12 if other else 10 + h, z_base(d, other, h))

    def z_copy(d, other, h, p, step):
        dst = z_slot(d, other, h, step < 0, z + step)
        return pltpu.make_async_remote_copy(src_ref=tot.at[home(d, other, h), part(p)], dst_ref=z_in.at[dst, part(p)], send_sem=zs_sem.at[z_base(d, other, h), p], recv_sem=zr_sem.at[dst, p], device_id={"ep": (me + 4 * step + GROUP) % GROUP})

    def z_add(d, other, h, p, step):
        src, w = z_slot(d, other, h, step < 0, z), home(d, other, h)
        pltpu.make_async_remote_copy(src_ref=tot.at[w, part(p)], dst_ref=z_in.at[src, part(p)], send_sem=zs_sem.at[z_base(d, other, h), p], recv_sem=zr_sem.at[src, p], device_id={"ep": me}).wait_recv()
        tot[w, part(p)] = tot[w, part(p)] + z_in[src, part(p)]

    def y_copy(d, h, p):
        i = mirror(z, d) * 2 + h
        return pltpu.make_async_remote_copy(src_ref=tot.at[home(d, 1, h), part(p)], dst_ref=y_in.at[i, part(p)], send_sem=ys.at[i, p], recv_sem=yrs.at[i, p], device_id={"ep": ynb})

    def y_add(d, h, p):
        y_copy(d, h, p).wait_recv()
        w = home(d, 0, h)
        tot[w, part(p)] = tot[w, part(p)] + y_in[mirror(z, d) * 2 + h, part(p)]

    def y_start(d, h):
        for p in HALVES:
            y_copy(d, h, p).start()

    def start_up(d, other, h):
        for p in HALVES:
            z_copy(d, other, h, p, way).start()

    def pass_up(d, other, h, p):
        z_add(d, other, h, p, way)
        z_copy(d, other, h, p, way).start()

    def y_up(d, h, p):
        y_add(d, h, p)
        z_copy(d, OWN, h, p, way).start()

    def y_chain(d, h, p):
        y_add(d, h, p)
        pass_up(d, OWN, h, p)

    def y_down(d, h, p):
        y_add(d, h, p)
        z_add(d, OWN, h, p, -way)
        z_copy(d, OWN, h, p, -way).start()

    def swap(chip, slot):
        return pltpu.make_async_remote_copy(src_ref=r_send.at[slot], dst_ref=r_recv.at[chip], send_sem=rs.at[chip], recv_sem=rr.at[chip], device_id={"ep": sib})

    def make(t):
        slot = t % 2
        d, yy = chip_of(t)
        chip = d * 2 + yy
        for p in HALVES:
            arrive(chip * 2 + 1 - c, p)
        rows = rows_of(chip)
        for cp in h_loads(t):
            cp.wait()
        if t < 7:
            for cp in h_loads(t + 1):
                cp.start()

        def per_expert(e, _):
            for h in CORES:
                s = chip * 2 + h
                hot = one_hot(meta[s, c * 2 + e], cap)
                gate = jnp.sum(jnp.where(hot, meta[s, 4 + c * 2 + e], 0.0), axis=1, keepdims=True)
                picked = jnp.dot(jnp.where(hot, 1.0, 0.0).astype(BF16), tok[s], preferred_element_type=F32)
                d_ref[h * cap:(h + 1) * cap, :] = (picked * gate).astype(BF16)
            g = dot_nt(d_ref[...], wd[e]).astype(BF16).astype(F32)
            h1 = hbuf[t % 2, 0, e].astype(F32)
            h3 = hbuf[t % 2, 1, e].astype(F32)
            sig = jax.nn.sigmoid(h1)
            act = h1 * sig
            a_ref[...] = (act * h3).astype(BF16)
            dh1[e, rows, :] = (g * h3 * sig * (1.0 + h1 * (1.0 - sig))).astype(BF16)
            dh3[e, rows, :] = (g * act).astype(BF16)
            for part, dest in ((1 - c, r_send), (c, r_own)):
                cols = pl.ds(pl.multiple_of(part * half, half), half)
                r = dot_nt(dh1[e, rows, :], wg[e, cols, :]) + dot_nt(dh3[e, rows, :], wu[e, cols, :])
                dest[slot, e] = r.astype(BF16)
            acc[e] += dot_tn(a_ref[...], d_ref[...])
            return 0

        lax.fori_loop(0, n_loc, per_expert, 0)
        swap(chip, slot).start()

    def combine(t):
        slot = t % 2
        d, yy = chip_of(t)
        chip = d * 2 + yy
        cp = swap(chip, slot)
        cp.wait_recv()
        for h in CORES:
            s = chip * 2 + h
            lanes = pl.ds(h * cap, cap)
            ids = (c * 2, c * 2 + 1, 2 - c * 2, 3 - c * 2)
            pick = jnp.concatenate([jnp.where(one_hot(meta[s, i], cap), 1.0, 0.0).astype(BF16) for i in ids], axis=0)
            vals = jnp.concatenate([r_own[slot, 0, lanes, :], r_own[slot, 1, lanes, :], r_recv[chip, 0, lanes, :], r_recv[chip, 1, lanes, :]], axis=0)
            tot[s] = dot_tn(pick, vals)
        cp.wait_send()

    def at_end(fn):
        pl.when(end)(fn)

    def at_mid(fn):
        pl.when(mid)(fn)

    make(0)
    combine(0)

    @at_end
    def _():
        for p in HALVES:
            y_arrival(Z0, p, True)
            relay(Z1, OWN, p, (CROSS, CORE))

    @at_mid
    def _():
        for p in HALVES:
            relay(Z0, OWN, p, (ONWARD, CORE))
            y_arrival(Z1, p)
            relay(Z2, OWN, p, (ONWARD, CROSS, CORE))

    def second(p):
        @at_end
        def _():
            y_arrival(Z1, p)
            relay(Z2, OWN, p, (CROSS, CORE))

        @at_mid
        def _():
            relay(Z0, OTHER, p, (ONWARD, CORE))
            y_arrival(Z2, p)
            relay(Z3, OWN, p, (ONWARD, CORE))

    def third(p):
        @at_end
        def _():
            y_arrival(Z2, p)
            relay(Z3, OWN, p, (CORE,))

        @at_mid
        def _():
            relay(Z3, OTHER, p, (ONWARD, CORE))

    make(1)
    make(2)
    second(LO)
    combine(1)
    combine(2)
    at_end(lambda: start_up(Z1, OWN, CORE0))
    second(HI)
    make(3)
    make(4)
    third(LO)
    combine(3)
    y_start(Z1, CORE1)
    combine(4)
    at_end(lambda: start_up(Z2, OWN, CORE0))
    at_mid(lambda: y_start(Z0, CORE0))
    third(HI)
    make(5)
    make(6)
    at_end(lambda: relay(Z3, OTHER, LO, (CORE,)))
    combine(5)

    @at_end
    def _():
        start_up(Z2, OTHER, CORE0)
        y_start(Z2, CORE1)

    combine(6)
    at_end(lambda: relay(Z3, OTHER, HI, (CORE,)))
    at_mid(lambda: pass_up(Z2, OWN, CORE0, LO))
    make(7)
    combine(7)
    y_start(Z3, CORE0)
    y_start(Z3, CORE1)
    at_end(lambda: y_start(Z0, CORE0))
    y_start(Z0, CORE1)
    at_mid(lambda: y_start(Z2, CORE1))

    width = xs.shape[2]

    def x_load(i):
        e, t = i // 4, i % 4
        return pltpu.make_async_copy(x_hbm.at[e, :, pl.ds(pl.multiple_of(t * width, width), width)], xs.at[i % 2], x_sem.at[i % 2])

    def w_out(i):
        e, t = i // 4, i % 4
        rows = pl.ds(pl.multiple_of(t * width, width), width)
        return (pltpu.make_async_copy(og.at[i % 2], gwg_hbm.at[e, rows, :], st_sem.at[i % 2, 0]),
                pltpu.make_async_copy(ou.at[i % 2], gwu_hbm.at[e, rows, :], st_sem.at[i % 2, 1]))

    def end_tail():
        y_up(Z3, CORE1, HI)
        start_up(Z1, OTHER, CORE0)
        for p in HALVES:
            y_up(Z1, CORE1, p)

    def end_first():
        for p in HALVES:
            y_up(Z2, CORE1, p)

    end_events = dict(enumerate((end_first, lambda: y_up(Z3, CORE0, LO), lambda: y_up(Z3, CORE0, HI), lambda: y_up(Z3, CORE1, LO), end_tail)))
    mid_events = {0: lambda: pass_up(Z2, OWN, CORE0, HI), 1: lambda: pass_up(Z2, OTHER, CORE0, LO), 2: lambda: pass_up(Z2, OTHER, CORE0, HI), 6: lambda: y_chain(Z3, CORE0, LO), 7: lambda: y_chain(Z3, CORE0, HI)}
    x_load(0).start()
    acc_out = pltpu.make_async_copy(acc, gwd_hbm, acc_sem.at[0])
    acc_out.start()

    def weights(i, _):
        x_load(i).wait()

        @pl.when(i < 7)
        def _():
            x_load(i + 1).start()

        @pl.when(i >= 2)
        def _():
            for cp in w_out(i - 2):
                cp.wait()

        e = i // 4
        og[i % 2] = dot_tn(xs[i % 2], dh1[e])
        ou[i % 2] = dot_tn(xs[i % 2], dh3[e])
        for cp in w_out(i):
            cp.start()
        for n, event in mid_events.items():
            pl.when(mid & (i == n))(event)
        for n, event in end_events.items():
            pl.when(end & (i == n))(event)
        return 0

    lax.fori_loop(0, 8, weights, 0)

    def cross(p):
        z_add(Z1, OTHER, CORE0, p, -way)
        z_add(Z1, OTHER, CORE0, p, way)
        y_copy(Z1, CORE0, p).start()

    @at_mid
    def _():
        y_down(Z0, CORE0, LO)
        y_chain(Z3, CORE1, LO)
        y_down(Z0, CORE0, HI)
        y_chain(Z3, CORE1, HI)
        y_down(Z0, CORE1, LO)
        cross(0)
        y_chain(Z2, CORE1, LO)
        y_down(Z0, CORE1, HI)
        cross(1)
        y_chain(Z2, CORE1, HI)

    def last(p):
        return pltpu.make_async_remote_copy(src_ref=f_send.at[part(p)], dst_ref=f_recv.at[part(p)], send_sem=fs.at[p], recv_sem=fr.at[p], device_id={"ep": sib})

    def finish(h, p):
        w = me - c + h
        i = z * 2 + h
        pltpu.make_async_remote_copy(src_ref=tot.at[w, part(p)], dst_ref=y_in.at[i, part(p)], send_sem=ys.at[i, p], recv_sem=yrs.at[i, p], device_id={"ep": ynb}).wait_recv()
        tot[w, part(p)] = tot[w, part(p)] + y_in[i, part(p)]
        at_end(lambda: z_add(Z0, OWN, h, p, -way))

        @at_mid
        def _():
            z_add(Z1, OWN, h, p, -way)
            z_add(Z1, OWN, h, p, way)

        @pl.when(c == h)
        def _():
            gx[part(p), h * half:(h + 1) * half] = tot[w, part(p)].astype(BF16)

        @pl.when(c != h)
        def _():
            f_send[part(p)] = tot[w, part(p)].astype(BF16)
            last(p).start()

    for p in HALVES:
        for h in CORES:
            finish(h, p)
    for p in HALVES:
        last(p).wait()
    for h in CORES:
        @pl.when(c == h)
        def _():
            gx[:, (1 - h) * half:(2 - h) * half] = f_recv[...]

    for cp, cond in own:
        cp.wait_send() if cond is None else pl.when(cond)(cp.wait_send)

    def drain(tokens, y_units, z_units):
        for p in HALVES:
            for d, other, links in tokens:
                for link in links:
                    put(home(d, other, c), link, me, p).wait_send()
            for d, h in y_units:
                y_copy(d, h, p).wait_send()
            for d, other, h in z_units:
                z_copy(d, other, h, p, way).wait_send()

    SENT = (CORE,)
    at_end(lambda: drain(
        ((Z0, OTHER, (ONWARD, CORE)), (Z1, OWN, (CROSS, CORE)), (Z1, OTHER, SENT), (Z2, OWN, (CROSS, CORE)), (Z2, OTHER, SENT), (Z3, OWN, SENT), (Z3, OTHER, SENT)),
        ((Z0, CORE0), (Z0, CORE1), (Z1, CORE1), (Z2, CORE1), (Z3, CORE0), (Z3, CORE1)),
        ((Z1, OWN, CORE0), (Z1, OTHER, CORE0), (Z2, OWN, CORE0), (Z2, OTHER, CORE0), (Z1, OWN, CORE1), (Z2, OWN, CORE1), (Z3, OWN, CORE0), (Z3, OWN, CORE1))))
    at_mid(lambda: drain(
        ((Z1, OTHER, SENT), (Z0, OWN, (ONWARD, CORE)), (Z0, OTHER, (ONWARD, CORE)), (Z2, OWN, (ONWARD, CROSS, CORE)), (Z2, OTHER, SENT), (Z3, OWN, (ONWARD, CORE)), (Z3, OTHER, (ONWARD, CORE))),
        ((Z0, CORE0), (Z0, CORE1), (Z1, CORE0), (Z1, CORE1), (Z2, CORE1), (Z3, CORE0), (Z3, CORE1)),
        ((Z2, OWN, CORE0), (Z2, OTHER, CORE0), (Z3, OWN, CORE0), (Z3, OWN, CORE1), (Z0, OWN, CORE0), (Z0, OWN, CORE1), (Z2, OWN, CORE1))))
    for k in PEERS:
        meta_copy(k).wait_send()
    for i in (6, 7):
        for cp in w_out(i):
            cp.wait()
    acc_out.wait()


def deliver_kernel(*refs):
    n = (len(refs) - 2) // 3
    src, dst, buf, (in_sem, out_sem) = refs[:n], refs[n:2 * n], refs[2 * n:3 * n], refs[3 * n:]
    pieces = []
    for s, d, b in zip(src, dst, buf):
        rows = s.shape[-2]
        parts = 2 if len(s.shape) == 3 else 1
        for lead in ([(e,) for e in range(s.shape[0])] if len(s.shape) == 3 else [()]):
            for k in range(parts):
                at = lead + (pl.ds(k * rows // parts, rows // parts),)
                i = len(pieces)
                pieces.append((pltpu.make_async_copy(s.at[at], b.at[at], in_sem.at[i]), pltpu.make_async_copy(b.at[at], d.at[at], out_sem.at[i])))
    for read, _ in pieces:
        read.start()
    for read, write in pieces:
        read.wait()
        write.start()
    for _, write in pieces:
        write.wait()


def deliver(arrays):
    n = 2 + 4 * (len(arrays) - 2)
    return pl.pallas_call(
        deliver_kernel,
        out_shape=tuple(jax.ShapeDtypeStruct(a.shape, a.dtype) for a in arrays),
        in_specs=[ANY] * len(arrays),
        out_specs=(ANY,) * len(arrays),
        scratch_shapes=[VMEM(a.shape, a.dtype) for a in arrays] + [DMA((n,)), DMA((n,))],
        compiler_params=pltpu.CompilerParams(vmem_limit_bytes=67043328),
        name="deliver",
    )(*arrays)


def solution(mesh):
    rows_spec = P(("dp", "ep"), None)
    cube_spec = P(("dp", "ep"), None, None)
    weight_spec = P("ep", None, None)

    def local_step(grad_y, gate_vals, topk_idx, slot_ids, pair_counts, y_routed, x_disp, h_gate, h_up, w_gate, w_up, w_down):
        n_loc, n_rows, ffn = h_gate.shape
        tok, dim = grad_y.shape
        top_k = topk_idx.shape[1]
        half = dim // 2
        cap = n_rows // 16
        shape = jax.ShapeDtypeStruct
        grad_x, grad_gate, grad_wdown, grad_wgate, grad_wup = pl.pallas_call(
            step_kernel,
            out_shape=(shape((tok, dim), BF16), shape((top_k, tok), F32), shape((n_loc, ffn, dim), F32), shape((n_loc, dim, ffn), F32), shape((n_loc, dim, ffn), F32)),
            in_specs=[VM, VM, VM, VM, pl.BlockSpec(memory_space=pltpu.SMEM)] + [ANY] * 7,
            out_specs=(VM, VM, ANY, ANY, ANY),
            scratch_shapes=[
                VMEM((16, tok, dim), BF16), VMEM((16, 8, 1, tok), F32), VMEM((8, 8, 1, tok), F32),
                VMEM((2, 2, n_loc, 2 * cap, ffn), BF16),
                VMEM((n_loc, ffn, dim), BF16), VMEM((n_loc, dim, ffn), BF16), VMEM((n_loc, dim, ffn), BF16),
                VMEM((2, n_rows, 256), BF16), VMEM((2, 256, dim), BF16),
                VMEM((2 * cap, dim), BF16), VMEM((2 * cap, ffn), BF16),
                VMEM((n_loc, n_rows, ffn), BF16), VMEM((n_loc, n_rows, ffn), BF16), VMEM((n_loc, ffn, dim), F32),
                VMEM((2, n_loc, 2 * cap, half), BF16), VMEM((2, n_loc, 2 * cap, half), BF16), VMEM((8, n_loc, 2 * cap, half), BF16),
                VMEM((16, tok, half), F32), VMEM((13, tok, half), F32), VMEM((8, tok, half), F32),
                VMEM((tok, half), BF16), VMEM((tok, half), BF16),
                VMEM((2, 256, ffn), F32), VMEM((2, 256, ffn), F32),
                DMA((3,)), DMA((2, 2)), DMA((2,)), DMA((2,)), DMA((2, 2)), DMA((1,)),
                DMA((16, 4, 2)), DMA((16, 2)), DMA((16,)), DMA((16,)), DMA((8,)), DMA((8,)), DMA((8, 2)), DMA((8, 2)), DMA((10, 2)), DMA((13, 2)), DMA((2,)), DMA((2,)),
            ],
            compiler_params=pltpu.CompilerParams(collective_id=1, has_side_effects=True, vmem_limit_bytes=67043328),
            name="step",
        )(grad_y, topk_idx.T, slot_ids.T, gate_vals.T, pair_counts, y_routed.reshape(tok * top_k, dim), h_gate, h_up, w_down, w_gate, w_up, x_disp)
        grad_wgate, grad_wup, grad_wdown, grad_x, grad_gate = deliver((grad_wgate, grad_wup, grad_wdown, grad_x, grad_gate))
        return grad_x, grad_gate.T, grad_wgate, grad_wup, grad_wdown

    return jax.shard_map(local_step, mesh=mesh, in_specs=(rows_spec, rows_spec, rows_spec, rows_spec, rows_spec, cube_spec, cube_spec, cube_spec, cube_spec, weight_spec, weight_spec, weight_spec), out_specs=(rows_spec, rows_spec, cube_spec, cube_spec, cube_spec), check_vma=False)
```

time: 156 us -> 147 us (0.942)
  Pallas kernels: 155 us -> 146 us
    pallas_call x1, Pallas kernels: 146 us -> 136 us  [local_step(): pl.pallas_call(step_kernel, out_shape=(shape((tok, dim), BF16), shape((to...]
where the time goes in v5:
time: 147 us
  Pallas kernels  146 us (99%)
    pallas_call x1, Pallas kernels, local_step(): pl.pallas_call(step_kernel, out_shape=(shape((tok, dim), BF16), shape((to...  136 us
    pallas_call x1, Pallas kernels, deliver(): pl.pallas_call(deliver_kernel, out_shape=tuple((jax.ShapeDtypeStruct(a.sh...  9.41 us

profile of v5, /device:TPU:19, one launch (start us, length us, event | category | flops | bytes accessed | tf_op | source)
XLA Modules:
  0.0 146.5 jit_solution(8999475424381303634)
XLA Ops:
  0.6 136.3 %step.1 = (bf16[256,1024]{1,0:T(8,128)(2,1)}, f32[8,256]{1,0:T(8,128)}, f32[2,512,1024]{2,1,0:T(8,128)}, f32[2,1024,512]{2,1,0:T(8,128)}, f32[2,1024,512]{2,1,0:T(8,128)}) custom-call(bf16[256,1024]{1,0:T(8,128)(2,1)} %gy.1, s32[8,256]{1,0:T(8,128)} %bitcast.6, s32[8,256]{1,0:T(8,128)} %bitcast.7, f32[8,256]{1,0:T(8,128)} %bitcast.8, s32[1,32]{1,0:T(1,128)} %counts.1, ...), custom_call_target="tpu_custom_call" | custom-call | tf_op jit(solution)/shard_map/step/pallas_call | solution.py:528
  136.9 9.4 %deliver.1 = (f32[2,1024,512]{2,1,0:T(8,128)}, f32[2,1024,512]{2,1,0:T(8,128)}, f32[2,512,1024]{2,1,0:T(8,128)}, bf16[256,1024]{1,0:T(8,128)(2,1)}, f32[8,256]{1,0:T(8,128)}) custom-call(f32[2,1024,512]{2,1,0:T(8,128)} %get-tuple-element.15.refs_0_, f32[2,1024,512]{2,1,0:T(8,128)} %get-tuple-element.16.refs_1_, f32[2,512,1024]{2,1,0:T(8,128)} %get-tuple-element.17.refs_2_, ...), custom_call_target="tpu_custom_call" | custom-call | tf_op jit(solution)/shard_map/deliver/pallas_call | solution.py:505

commit v6 on v5

--- a/solution.py
+++ b/solution.py
@@ -207,8 +207,16 @@
         z_add(d, OWN, h, p, -way)
         z_copy(d, OWN, h, p, -way).start()
 
-    def swap(chip, slot):
-        return pltpu.make_async_remote_copy(src_ref=r_send.at[slot], dst_ref=r_recv.at[chip], send_sem=rs.at[chip], recv_sem=rr.at[chip], device_id={"ep": sib})
+    def swap(chip, slot, e):
+        return pltpu.make_async_remote_copy(src_ref=r_send.at[slot, e], dst_ref=r_recv.at[chip, e], send_sem=rs.at[chip, e], recv_sem=rr.at[chip, e], device_id={"ep": sib})
+
+    def build_rows(chip, e):
+        for h in CORES:
+            s = chip * 2 + h
+            hot = one_hot(meta[s, c * 2 + e], cap)
+            gate = jnp.sum(jnp.where(hot, meta[s, 4 + c * 2 + e], 0.0), axis=1, keepdims=True)
+            picked = jnp.dot(jnp.where(hot, 1.0, 0.0).astype(BF16), tok[s], preferred_element_type=F32)
+            d_ref[h * cap:(h + 1) * cap, :] = (picked * gate).astype(BF16)
 
     def make(t):
         slot = t % 2
@@ -224,36 +232,32 @@
                 cp.start()
 
         def per_expert(e, _):
-            for h in CORES:
-                s = chip * 2 + h
-                hot = one_hot(meta[s, c * 2 + e], cap)
-                gate = jnp.sum(jnp.where(hot, meta[s, 4 + c * 2 + e], 0.0), axis=1, keepdims=True)
-                picked = jnp.dot(jnp.where(hot, 1.0, 0.0).astype(BF16), tok[s], preferred_element_type=F32)
-                d_ref[h * cap:(h + 1) * cap, :] = (picked * gate).astype(BF16)
+            build_rows(chip, e)
             g = dot_nt(d_ref[...], wd[e]).astype(BF16).astype(F32)
             h1 = hbuf[t % 2, 0, e].astype(F32)
             h3 = hbuf[t % 2, 1, e].astype(F32)
             sig = jax.nn.sigmoid(h1)
             act = h1 * sig
-            a_ref[...] = (act * h3).astype(BF16)
             dh1[e, rows, :] = (g * h3 * sig * (1.0 + h1 * (1.0 - sig))).astype(BF16)
             dh3[e, rows, :] = (g * act).astype(BF16)
-            for part, dest in ((1 - c, r_send), (c, r_own)):
-                cols = pl.ds(pl.multiple_of(part * half, half), half)
-                r = dot_nt(dh1[e, rows, :], wg[e, cols, :]) + dot_nt(dh3[e, rows, :], wu[e, cols, :])
-                dest[slot, e] = r.astype(BF16)
-            acc[e] += dot_tn(a_ref[...], d_ref[...])
+
+            def ret_rows(side):
+                cols = pl.ds(pl.multiple_of(side * half, half), half)
+                return (dot_nt(dh1[e, rows, :], wg[e, cols, :]) + dot_nt(dh3[e, rows, :], wu[e, cols, :])).astype(BF16)
+
+            r_send[slot, e] = ret_rows(1 - c)
+            swap(chip, slot, e).start()
+            r_own[slot, e] = ret_rows(c)
             return 0
 
         lax.fori_loop(0, n_loc, per_expert, 0)
-        swap(chip, slot).start()
 
     def combine(t):
         slot = t % 2
         d, yy = chip_of(t)
         chip = d * 2 + yy
-        cp = swap(chip, slot)
-        cp.wait_recv()
+        for e in range(n_loc):
+            swap(chip, slot, e).wait_recv()
         for h in CORES:
             s = chip * 2 + h
             lanes = pl.ds(h * cap, cap)
@@ -261,7 +265,8 @@
             pick = jnp.concatenate([jnp.where(one_hot(meta[s, i], cap), 1.0, 0.0).astype(BF16) for i in ids], axis=0)
             vals = jnp.concatenate([r_own[slot, 0, lanes, :], r_own[slot, 1, lanes, :], r_recv[chip, 0, lanes, :], r_recv[chip, 1, lanes, :]], axis=0)
             tot[s] = dot_tn(pick, vals)
-        cp.wait_send()
+        for e in range(n_loc):
+            swap(chip, slot, e).wait_send()
 
     def at_end(fn):
         pl.when(end)(fn)
@@ -368,9 +373,32 @@
 
     end_events = dict(enumerate((end_first, lambda: y_up(Z3, CORE0, LO), lambda: y_up(Z3, CORE0, HI), lambda: y_up(Z3, CORE1, LO), end_tail)))
     mid_events = {0: lambda: pass_up(Z2, OWN, CORE0, HI), 1: lambda: pass_up(Z2, OTHER, CORE0, LO), 2: lambda: pass_up(Z2, OTHER, CORE0, HI), 6: lambda: y_chain(Z3, CORE0, LO), 7: lambda: y_chain(Z3, CORE0, HI)}
+    def tail_loads(i):
+        rows = rows_of(i)
+        return [pltpu.make_async_copy(src.at[:, rows, :], hbuf.at[i % 2, n], h_sem.at[i % 2, n]) for n, src in enumerate((hg_hbm, hu_hbm))]
+
     x_load(0).start()
-    acc_out = pltpu.make_async_copy(acc, gwd_hbm, acc_sem.at[0])
-    acc_out.start()
+    for cp in tail_loads(0):
+        cp.start()
+
+    def down_grad(i):
+        for cp in tail_loads(i):
+            cp.wait()
+
+        @pl.when(i < 7)
+        def _():
+            for cp in tail_loads(i + 1):
+                cp.start()
+
+        def per_expert(e, _):
+            build_rows(i, e)
+            h1 = hbuf[i % 2, 0, e].astype(F32)
+            a_ref[...] = (h1 * jax.nn.sigmoid(h1) * hbuf[i % 2, 1, e].astype(F32)).astype(BF16)
+            acc[e] += dot_tn(a_ref[...], d_ref[...])
+            return 0
+
+        lax.fori_loop(0, n_loc, per_expert, 0)
+
 
     def weights(i, _):
         x_load(i).wait()
@@ -389,6 +417,7 @@
         ou[i % 2] = dot_tn(xs[i % 2], dh3[e])
         for cp in w_out(i):
             cp.start()
+        down_grad(i)
         for n, event in mid_events.items():
             pl.when(mid & (i == n))(event)
         for n, event in end_events.items():
@@ -396,6 +425,8 @@
         return 0
 
     lax.fori_loop(0, 8, weights, 0)
+    acc_out = pltpu.make_async_copy(acc, gwd_hbm, acc_sem.at[0])
+    acc_out.start()
 
     def cross(p):
         z_add(Z1, OTHER, CORE0, p, -way)
@@ -542,7 +573,7 @@
                 VMEM((tok, half), BF16), VMEM((tok, half), BF16),
                 VMEM((2, 256, ffn), F32), VMEM((2, 256, ffn), F32),
                 DMA((3,)), DMA((2, 2)), DMA((2,)), DMA((2,)), DMA((2, 2)), DMA((1,)),
-                DMA((16, 4, 2)), DMA((16, 2)), DMA((16,)), DMA((16,)), DMA((8,)), DMA((8,)), DMA((8, 2)), DMA((8, 2)), DMA((10, 2)), DMA((13, 2)), DMA((2,)), DMA((2,)),
+                DMA((16, 4, 2)), DMA((16, 2)), DMA((16,)), DMA((16,)), DMA((8, n_loc)), DMA((8, n_loc)), DMA((8, 2)), DMA((8, 2)), DMA((10, 2)), DMA((13, 2)), DMA((2,)), DMA((2,)),
             ],
             compiler_params=pltpu.CompilerParams(collective_id=1, has_side_effects=True, vmem_limit_bytes=67043328),
             name="step",

time: 147 us -> 145 us (0.986)
  Pallas kernels: 146 us -> 144 us
    pallas_call x1, Pallas kernels: 136 us -> 134 us  [local_step(): pl.pallas_call(step_kernel, out_shape=(shape((tok, dim), BF16), shape((to...]
where the time goes in v6:
time: 145 us
  Pallas kernels  144 us (99%)
    pallas_call x1, Pallas kernels, local_step(): pl.pallas_call(step_kernel, out_shape=(shape((tok, dim), BF16), shape((to...  134 us
    pallas_call x1, Pallas kernels, deliver(): pl.pallas_call(deliver_kernel, out_shape=tuple((jax.ShapeDtypeStruct(a.sh...  9.41 us

profile of v6, /device:TPU:19, one launch (start us, length us, event | category | flops | bytes accessed | tf_op | source)
XLA Modules:
  0.0 144.7 jit_solution(16884348513222044528)
XLA Ops:
  0.6 134.5 %step.1 = (bf16[256,1024]{1,0:T(8,128)(2,1)}, f32[8,256]{1,0:T(8,128)}, f32[2,512,1024]{2,1,0:T(8,128)}, f32[2,1024,512]{2,1,0:T(8,128)}, f32[2,1024,512]{2,1,0:T(8,128)}) custom-call(bf16[256,1024]{1,0:T(8,128)(2,1)} %gy.1, s32[8,256]{1,0:T(8,128)} %bitcast.6, s32[8,256]{1,0:T(8,128)} %bitcast.7, f32[8,256]{1,0:T(8,128)} %bitcast.8, s32[1,32]{1,0:T(1,128)} %counts.1, ...), custom_call_target="tpu_custom_call" | custom-call | tf_op jit(solution)/shard_map/step/pallas_call | solution.py:559
  135.1 9.4 %deliver.1 = (f32[2,1024,512]{2,1,0:T(8,128)}, f32[2,1024,512]{2,1,0:T(8,128)}, f32[2,512,1024]{2,1,0:T(8,128)}, bf16[256,1024]{1,0:T(8,128)(2,1)}, f32[8,256]{1,0:T(8,128)}) custom-call(f32[2,1024,512]{2,1,0:T(8,128)} %get-tuple-element.15.refs_0_, f32[2,1024,512]{2,1,0:T(8,128)} %get-tuple-element.16.refs_1_, f32[2,512,1024]{2,1,0:T(8,128)} %get-tuple-element.17.refs_2_, ...), custom_call_target="tpu_custom_call" | custom-call | tf_op jit(solution)/shard_map/deliver/pallas_call | solution.py:536

commit v7 on v6

--- a/solution.py
+++ b/solution.py
@@ -136,9 +136,6 @@
         return 0
 
     lax.fori_loop(0, 8, gate_block, 0)
-    for k in PEERS:
-        src = (me + k) % GROUP
-        pltpu.make_async_remote_copy(src_ref=meta_out.at[0], dst_ref=meta.at[src], send_sem=m_send.at[k], recv_sem=m_recv.at[src], device_id={"ep": src}).wait_recv()
     for cp in w_loads:
         cp.wait()
 
@@ -222,6 +219,13 @@
         slot = t % 2
         d, yy = chip_of(t)
         chip = d * 2 + yy
+        for h in CORES:
+            src = chip * 2 + h
+
+            def table(src=src):
+                pltpu.make_async_remote_copy(src_ref=meta_out.at[0], dst_ref=meta.at[src], send_sem=m_send.at[0], recv_sem=m_recv.at[src], device_id={"ep": src}).wait_recv()
+
+            table() if t else pl.when(src != me)(table)
         for p in HALVES:
             arrive(chip * 2 + 1 - c, p)
         rows = rows_of(chip)

time: 145 us -> 138 us (0.952)
  Pallas kernels: 144 us -> 136 us
    pallas_call x1, Pallas kernels: 134 us -> 127 us  [local_step(): pl.pallas_call(step_kernel, out_shape=(shape((tok, dim), BF16), shape((to...]
where the time goes in v7:
time: 138 us; the launch traced here: 137 us
  Pallas kernels  136 us (99%)
    pallas_call x1, Pallas kernels, local_step(): pl.pallas_call(step_kernel, out_shape=(shape((tok, dim), BF16), shape((to...  127 us
    pallas_call x1, Pallas kernels, deliver(): pl.pallas_call(deliver_kernel, out_shape=tuple((jax.ShapeDtypeStruct(a.sh...  9.41 us

profile of v7, /device:TPU:19, one launch (start us, length us, event | category | flops | bytes accessed | tf_op | source)
XLA Modules:
  0.0 137.2 jit_solution(6013632045767460792)
XLA Ops:
  0.6 127.0 %step.1 = (bf16[256,1024]{1,0:T(8,128)(2,1)}, f32[8,256]{1,0:T(8,128)}, f32[2,512,1024]{2,1,0:T(8,128)}, f32[2,1024,512]{2,1,0:T(8,128)}, f32[2,1024,512]{2,1,0:T(8,128)}) custom-call(bf16[256,1024]{1,0:T(8,128)(2,1)} %gy.1, s32[8,256]{1,0:T(8,128)} %bitcast.6, s32[8,256]{1,0:T(8,128)} %bitcast.7, f32[8,256]{1,0:T(8,128)} %bitcast.8, s32[1,32]{1,0:T(1,128)} %counts.1, ...), custom_call_target="tpu_custom_call" | custom-call | tf_op jit(solution)/shard_map/step/pallas_call | solution.py:563
  127.6 9.4 %deliver.1 = (f32[2,1024,512]{2,1,0:T(8,128)}, f32[2,1024,512]{2,1,0:T(8,128)}, f32[2,512,1024]{2,1,0:T(8,128)}, bf16[256,1024]{1,0:T(8,128)(2,1)}, f32[8,256]{1,0:T(8,128)}) custom-call(f32[2,1024,512]{2,1,0:T(8,128)} %get-tuple-element.15.refs_0_, f32[2,1024,512]{2,1,0:T(8,128)} %get-tuple-element.16.refs_1_, f32[2,512,1024]{2,1,0:T(8,128)} %get-tuple-element.17.refs_2_, ...), custom_call_target="tpu_custom_call" | custom-call | tf_op jit(solution)/shard_map/deliver/pallas_call | solution.py:540

commit v8 on v7

--- a/solution.py
+++ b/solution.py
@@ -39,9 +39,9 @@
     return slot == lax.broadcasted_iota(jnp.int32, (cap, slot.shape[1]), 0).astype(F32)
 
 
-def step_kernel(gy, idx_t, slot_t, gate_t, counts, yr_hbm, hg_hbm, hu_hbm, wd_hbm, wg_hbm, wu_hbm, x_hbm, gx, gg, gwd_hbm, gwg_hbm, gwu_hbm,
-                tok, meta, meta_out, hbuf, wd, wg, wu, xs, yr, d_ref, a_ref, dh1, dh3, acc, r_own, r_send, r_recv, tot, z_in, y_in, f_send, f_recv, og, ou,
-                w_sem, h_sem, x_sem, g_sem, st_sem, acc_sem, send, recv, m_send, m_recv, rs, rr, ys, yrs, zs_sem, zr_sem, fs, fr):
+def step_kernel(gy_hbm, idx_hbm, slot_hbm, gate_hbm, counts_hbm, yr_hbm, hg_hbm, hu_hbm, wd_hbm, wg_hbm, wu_hbm, x_hbm, gx, gg, gwd_hbm, gwg_hbm, gwu_hbm,
+                gy, idx_t, slot_t, gate_t, counts, tok, meta, meta_out, hbuf, wd, wg, wu, xs, yr, d_ref, a_ref, dh1, dh3, acc, r_own, r_send, r_recv, tot, z_in, y_in, f_send, f_recv, og, ou,
+                in_sem, w_sem, h_sem, x_sem, g_sem, st_sem, acc_sem, send, recv, m_send, m_recv, rs, rr, ys, yrs, zs_sem, zr_sem, fs, fr):
     me, z, y, c = position()
     n_loc, n_rows, ffn = dh1.shape
     cap = n_rows // 16
@@ -57,6 +57,13 @@
     up = (me + 4 * way + GROUP) % GROUP
     down = (me - 4 * way + GROUP) % GROUP
 
+    barrier = pltpu.get_barrier_semaphore()
+    for k in PEERS:
+        pl.semaphore_signal(barrier, inc=1, device_id={"ep": (me + k) % GROUP})
+    inputs = [pltpu.make_async_copy(src, dst, in_sem.at[i]) for i, (src, dst) in enumerate(((gy_hbm, gy), (idx_hbm, idx_t), (slot_hbm, slot_t), (gate_hbm, gate_t), (counts_hbm, counts)))]
+    for cp in inputs:
+        cp.start()
+
     order = (((Z0, OWN), (Z1, OWN)), ((Z0, OTHER), (Z0, OWN)), ((Z1, OWN), (Z2, OWN)), ((Z1, OTHER), (Z1, OTHER)), ((Z2, OWN), (Z0, OTHER)), ((Z2, OTHER), (Z3, OWN)), ((Z3, OWN), (Z2, OTHER)), ((Z3, OTHER), (Z3, OTHER)))
 
     def chip_of(t):
@@ -73,18 +80,37 @@
         return [pltpu.make_async_copy(src.at[:, rows, :], hbuf.at[t % 2, i], h_sem.at[t % 2, i]) for i, src in enumerate((hg_hbm, hu_hbm))]
 
     w_loads = [pltpu.make_async_copy(src, dst, w_sem.at[i]) for i, (src, dst) in enumerate(((wd_hbm, wd), (wg_hbm, wg), (wu_hbm, wu)))]
+    def yr_load(i):
+        return pltpu.make_async_copy(yr_hbm.at[pl.ds(pl.multiple_of(i * 256, 256), 256), :], yr.at[i % 2], g_sem.at[i % 2])
+
+
+    part_rows = gy.shape[0] // 2
+
+    def part(p):
+        return pl.ds(p * part_rows, part_rows)
+
+    def put(slot, link, to, p, src=None):
+        src = tok.at[slot, part(p)] if src is None else src
+        return pltpu.make_async_remote_copy(src_ref=src, dst_ref=tok.at[slot, part(p)], send_sem=send.at[slot, link, p], recv_sem=recv.at[slot, p], device_id={"ep": to})
+
+    def arrive(slot, p):
+        put(slot, 0, me, p).wait_recv()
+
+    def meta_copy(k):
+        to = (me + k) % GROUP
+        return pltpu.make_async_remote_copy(src_ref=meta_out.at[to // 2], dst_ref=meta.at[me], send_sem=m_send.at[k], recv_sem=m_recv.at[me], device_id={"ep": to})
+
+    own = [(put(me, link, to, p, gy.at[part(p)]), cond) for p in HALVES for link, to, cond in ((ONWARD, up, None), (DOWN, down, mid), (CROSS, ynb, None), (CORE, sib, None))]
+    inputs[0].wait()
     for cp in h_loads(0) + w_loads:
         cp.start()
-
-    def yr_load(i):
-        return pltpu.make_async_copy(yr_hbm.at[pl.ds(pl.multiple_of(i * 256, 256), 256), :], yr.at[i % 2], g_sem.at[i % 2])
-
     yr_load(0).start()
-
-    barrier = pltpu.get_barrier_semaphore()
-    for k in PEERS:
-        pl.semaphore_signal(barrier, inc=1, device_id={"ep": (me + k) % GROUP})
-
+    pl.semaphore_wait(barrier, GROUP - 1)
+    for cp, cond in own:
+        cp.start() if cond is None else pl.when(cond)(cp.start)
+
+    for cp in inputs[1:]:
+        cp.wait()
     idx, slots, gates = idx_t[...], slot_t[...], gate_t[...]
     for e in range(n_exp):
         hit = idx == e
@@ -92,27 +118,6 @@
         slot = jnp.where(slot < counts[0, e], slot, -1)
         meta_out[e // 4, e % 4] = slot.astype(F32)
         meta_out[e // 4, 4 + e % 4] = jnp.sum(jnp.where(hit, gates, 0.0), axis=0, keepdims=True)
-    pl.semaphore_wait(barrier, 15)
-
-    part_rows = gy.shape[0] // 2
-
-    def part(p):
-        return pl.ds(p * part_rows, part_rows)
-
-    def put(slot, link, to, p, src=None):
-        src = tok.at[slot, part(p)] if src is None else src
-        return pltpu.make_async_remote_copy(src_ref=src, dst_ref=tok.at[slot, part(p)], send_sem=send.at[slot, link, p], recv_sem=recv.at[slot, p], device_id={"ep": to})
-
-    def arrive(slot, p):
-        put(slot, 0, me, p).wait_recv()
-
-    def meta_copy(k):
-        to = (me + k) % GROUP
-        return pltpu.make_async_remote_copy(src_ref=meta_out.at[to // 2], dst_ref=meta.at[me], send_sem=m_send.at[k], recv_sem=m_recv.at[me], device_id={"ep": to})
-
-    own = [(put(me, link, to, p, gy.at[part(p)]), cond) for p in HALVES for link, to, cond in ((ONWARD, up, None), (DOWN, down, mid), (CROSS, ynb, None), (CORE, sib, None))]
-    for cp, cond in own:
-        cp.start() if cond is None else pl.when(cond)(cp.start)
     for k in PEERS:
         meta_copy(k).start()
     tok[me] = gy[...]
@@ -563,9 +568,10 @@
         grad_x, grad_gate, grad_wdown, grad_wgate, grad_wup = pl.pallas_call(
             step_kernel,
             out_shape=(shape((tok, dim), BF16), shape((top_k, tok), F32), shape((n_loc, ffn, dim), F32), shape((n_loc, dim, ffn), F32), shape((n_loc, dim, ffn), F32)),
-            in_specs=[VM, VM, VM, VM, pl.BlockSpec(memory_space=pltpu.SMEM)] + [ANY] * 7,
+            in_specs=[ANY] * 12,
             out_specs=(VM, VM, ANY, ANY, ANY),
             scratch_shapes=[
+                VMEM((tok, dim), BF16), VMEM((top_k, tok), jnp.int32), VMEM((top_k, tok), jnp.int32), VMEM((top_k, tok), F32), pltpu.SMEM(pair_counts.shape, jnp.int32),
                 VMEM((16, tok, dim), BF16), VMEM((16, 8, 1, tok), F32), VMEM((8, 8, 1, tok), F32),
                 VMEM((2, 2, n_loc, 2 * cap, ffn), BF16),
                 VMEM((n_loc, ffn, dim), BF16), VMEM((n_loc, dim, ffn), BF16), VMEM((n_loc, dim, ffn), BF16),
@@ -576,7 +582,7 @@
                 VMEM((16, tok, half), F32), VMEM((13, tok, half), F32), VMEM((8, tok, half), F32),
                 VMEM((tok, half), BF16), VMEM((tok, half), BF16),
                 VMEM((2, 256, ffn), F32), VMEM((2, 256, ffn), F32),
-                DMA((3,)), DMA((2, 2)), DMA((2,)), DMA((2,)), DMA((2, 2)), DMA((1,)),
+                DMA((5,)), DMA((3,)), DMA((2, 2)), DMA((2,)), DMA((2,)), DMA((2, 2)), DMA((1,)),
                 DMA((16, 4, 2)), DMA((16, 2)), DMA((16,)), DMA((16,)), DMA((8, n_loc)), DMA((8, n_loc)), DMA((8, 2)), DMA((8, 2)), DMA((10, 2)), DMA((13, 2)), DMA((2,)), DMA((2,)),
             ],
             compiler_params=pltpu.CompilerParams(collective_id=1, has_side_effects=True, vmem_limit_bytes=67043328),

time: 138 us -> 138 us (level)
  no operation moved by 1% of the time
where the time goes in v8:
time: 138 us; the launch traced here: 137 us
  Pallas kernels  136 us (99%)
    pallas_call x1, Pallas kernels, local_step(): pl.pallas_call(step_kernel, out_shape=(shape((tok, dim), BF16), shape((to...  127 us
    pallas_call x1, Pallas kernels, deliver(): pl.pallas_call(deliver_kernel, out_shape=tuple((jax.ShapeDtypeStruct(a.sh...  9.41 us

profile of v8, /device:TPU:19, one launch (start us, length us, event | category | flops | bytes accessed | tf_op | source)
XLA Modules:
  0.0 137.0 jit_solution(7685983670518399359)
XLA Ops:
  0.6 126.8 %step.1 = (bf16[256,1024]{1,0:T(8,128)(2,1)}, f32[8,256]{1,0:T(8,128)}, f32[2,512,1024]{2,1,0:T(8,128)}, f32[2,1024,512]{2,1,0:T(8,128)}, f32[2,1024,512]{2,1,0:T(8,128)}) custom-call(bf16[256,1024]{1,0:T(8,128)(2,1)} %gy_hbm.1, s32[8,256]{1,0:T(8,128)} %bitcast.6, s32[8,256]{1,0:T(8,128)} %bitcast.7, f32[8,256]{1,0:T(8,128)} %bitcast.8, ...), custom_call_target="tpu_custom_call" | custom-call | tf_op jit(solution)/shard_map/step/pallas_call | solution.py:568
  127.4 9.4 %deliver.1 = (f32[2,1024,512]{2,1,0:T(8,128)}, f32[2,1024,512]{2,1,0:T(8,128)}, f32[2,512,1024]{2,1,0:T(8,128)}, bf16[256,1024]{1,0:T(8,128)(2,1)}, f32[8,256]{1,0:T(8,128)}) custom-call(f32[2,1024,512]{2,1,0:T(8,128)} %get-tuple-element.15.refs_0_, f32[2,1024,512]{2,1,0:T(8,128)} %get-tuple-element.16.refs_1_, f32[2,512,1024]{2,1,0:T(8,128)} %get-tuple-element.17.refs_2_, ...), custom_call_target="tpu_custom_call" | custom-call | tf_op jit(solution)/shard_map/deliver/pallas_call | solution.py:545

commit v9 on v8

--- a/solution.py
+++ b/solution.py
@@ -40,8 +40,8 @@
 
 
 def step_kernel(gy_hbm, idx_hbm, slot_hbm, gate_hbm, counts_hbm, yr_hbm, hg_hbm, hu_hbm, wd_hbm, wg_hbm, wu_hbm, x_hbm, gx, gg, gwd_hbm, gwg_hbm, gwu_hbm,
-                gy, idx_t, slot_t, gate_t, counts, tok, meta, meta_out, hbuf, wd, wg, wu, xs, yr, d_ref, a_ref, dh1, dh3, acc, r_own, r_send, r_recv, tot, z_in, y_in, f_send, f_recv, og, ou,
-                in_sem, w_sem, h_sem, x_sem, g_sem, st_sem, acc_sem, send, recv, m_send, m_recv, rs, rr, ys, yrs, zs_sem, zr_sem, fs, fr):
+                gy, idx_t, slot_t, gate_t, counts, tok, meta, meta_out, hbuf, wd, wg, wu, xs, yr, d_ref, a_ref, dh1, dh3, acc, r_own, r_send, r_recv, tot, z_in, y_in, f_send, f_recv, f_own, og, ou,
+                in_sem, w_sem, h_sem, x_sem, g_sem, st_sem, acc_sem, send, recv, m_send, m_recv, rs, rr, ys, yrs, zs_sem, zr_sem, fs, fr, gx_sem):
     me, z, y, c = position()
     n_loc, n_rows, ffn = dh1.shape
     cap = n_rows // 16
@@ -455,8 +455,38 @@
         cross(1)
         y_chain(Z2, CORE1, HI)
 
+    for cp, cond in own:
+        cp.wait_send() if cond is None else pl.when(cond)(cp.wait_send)
+
+    def drain_tokens(*tokens):
+        for p in HALVES:
+            for d, other, links in tokens:
+                for link in links:
+                    put(home(d, other, c), link, me, p).wait_send()
+
+    def drain_units(y_units, z_units):
+        for p in HALVES:
+            for d, h in y_units:
+                y_copy(d, h, p).wait_send()
+            for d, other, h in z_units:
+                z_copy(d, other, h, p, way).wait_send()
+
+    SENT = (CORE,)
+    at_end(lambda: drain_tokens((Z0, OTHER, (ONWARD, CORE)), (Z1, OWN, (CROSS, CORE)), (Z1, OTHER, SENT), (Z2, OWN, (CROSS, CORE)), (Z2, OTHER, SENT), (Z3, OWN, SENT), (Z3, OTHER, SENT)))
+    at_mid(lambda: drain_tokens((Z1, OTHER, SENT), (Z0, OWN, (ONWARD, CORE)), (Z0, OTHER, (ONWARD, CORE)), (Z2, OWN, (ONWARD, CROSS, CORE)), (Z2, OTHER, SENT), (Z3, OWN, (ONWARD, CORE)), (Z3, OTHER, (ONWARD, CORE))))
+    for k in PEERS:
+        meta_copy(k).wait_send()
+    for i in (6, 7):
+        for cp in w_out(i):
+            cp.wait()
+    acc_out.wait()
+
     def last(p):
         return pltpu.make_async_remote_copy(src_ref=f_send.at[part(p)], dst_ref=f_recv.at[part(p)], send_sem=fs.at[p], recv_sem=fr.at[p], device_id={"ep": sib})
+
+    def gx_copy(side, p):
+        cols = pl.ds(pl.multiple_of((c + side * (1 - 2 * c)) * half, half), half)
+        return pltpu.make_async_copy((f_recv if side else f_own).at[part(p)], gx.at[part(p), cols], gx_sem.at[side, p])
 
     def finish(h, p):
         w = me - c + h
@@ -472,7 +502,8 @@
 
         @pl.when(c == h)
         def _():
-            gx[part(p), h * half:(h + 1) * half] = tot[w, part(p)].astype(BF16)
+            f_own[part(p)] = tot[w, part(p)].astype(BF16)
+            gx_copy(OWN, p).start()
 
         @pl.when(c != h)
         def _():
@@ -484,39 +515,12 @@
             finish(h, p)
     for p in HALVES:
         last(p).wait()
-    for h in CORES:
-        @pl.when(c == h)
-        def _():
-            gx[:, (1 - h) * half:(2 - h) * half] = f_recv[...]
-
-    for cp, cond in own:
-        cp.wait_send() if cond is None else pl.when(cond)(cp.wait_send)
-
-    def drain(tokens, y_units, z_units):
-        for p in HALVES:
-            for d, other, links in tokens:
-                for link in links:
-                    put(home(d, other, c), link, me, p).wait_send()
-            for d, h in y_units:
-                y_copy(d, h, p).wait_send()
-            for d, other, h in z_units:
-                z_copy(d, other, h, p, way).wait_send()
-
-    SENT = (CORE,)
-    at_end(lambda: drain(
-        ((Z0, OTHER, (ONWARD, CORE)), (Z1, OWN, (CROSS, CORE)), (Z1, OTHER, SENT), (Z2, OWN, (CROSS, CORE)), (Z2, OTHER, SENT), (Z3, OWN, SENT), (Z3, OTHER, SENT)),
-        ((Z0, CORE0), (Z0, CORE1), (Z1, CORE1), (Z2, CORE1), (Z3, CORE0), (Z3, CORE1)),
-        ((Z1, OWN, CORE0), (Z1, OTHER, CORE0), (Z2, OWN, CORE0), (Z2, OTHER, CORE0), (Z1, OWN, CORE1), (Z2, OWN, CORE1), (Z3, OWN, CORE0), (Z3, OWN, CORE1))))
-    at_mid(lambda: drain(
-        ((Z1, OTHER, SENT), (Z0, OWN, (ONWARD, CORE)), (Z0, OTHER, (ONWARD, CORE)), (Z2, OWN, (ONWARD, CROSS, CORE)), (Z2, OTHER, SENT), (Z3, OWN, (ONWARD, CORE)), (Z3, OTHER, (ONWARD, CORE))),
-        ((Z0, CORE0), (Z0, CORE1), (Z1, CORE0), (Z1, CORE1), (Z2, CORE1), (Z3, CORE0), (Z3, CORE1)),
-        ((Z2, OWN, CORE0), (Z2, OTHER, CORE0), (Z3, OWN, CORE0), (Z3, OWN, CORE1), (Z0, OWN, CORE0), (Z0, OWN, CORE1), (Z2, OWN, CORE1))))
-    for k in PEERS:
-        meta_copy(k).wait_send()
-    for i in (6, 7):
-        for cp in w_out(i):
-            cp.wait()
-    acc_out.wait()
+        gx_copy(OTHER, p).start()
+    at_end(lambda: drain_units(((Z0, CORE0), (Z0, CORE1), (Z1, CORE1), (Z2, CORE1), (Z3, CORE0), (Z3, CORE1)), ((Z1, OWN, CORE0), (Z1, OTHER, CORE0), (Z2, OWN, CORE0), (Z2, OTHER, CORE0), (Z1, OWN, CORE1), (Z2, OWN, CORE1), (Z3, OWN, CORE0), (Z3, OWN, CORE1))))
+    at_mid(lambda: drain_units(((Z0, CORE0), (Z0, CORE1), (Z1, CORE0), (Z1, CORE1), (Z2, CORE1), (Z3, CORE0), (Z3, CORE1)), ((Z2, OWN, CORE0), (Z2, OTHER, CORE0), (Z3, OWN, CORE0), (Z3, OWN, CORE1), (Z0, OWN, CORE0), (Z0, OWN, CORE1), (Z2, OWN, CORE1))))
+    for p in HALVES:
+        for side in (OWN, OTHER):
+            gx_copy(side, p).wait()
 
 
 def deliver_kernel(*refs):
@@ -569,7 +573,7 @@
             step_kernel,
             out_shape=(shape((tok, dim), BF16), shape((top_k, tok), F32), shape((n_loc, ffn, dim), F32), shape((n_loc, dim, ffn), F32), shape((n_loc, dim, ffn), F32)),
             in_specs=[ANY] * 12,
-            out_specs=(VM, VM, ANY, ANY, ANY),
+            out_specs=(ANY, VM, ANY, ANY, ANY),
             scratch_shapes=[
                 VMEM((tok, dim), BF16), VMEM((top_k, tok), jnp.int32), VMEM((top_k, tok), jnp.int32), VMEM((top_k, tok), F32), pltpu.SMEM(pair_counts.shape, jnp.int32),
                 VMEM((16, tok, dim), BF16), VMEM((16, 8, 1, tok), F32), VMEM((8, 8, 1, tok), F32),
@@ -580,10 +584,10 @@
                 VMEM((n_loc, n_rows, ffn), BF16), VMEM((n_loc, n_rows, ffn), BF16), VMEM((n_loc, ffn, dim), F32),
                 VMEM((2, n_loc, 2 * cap, half), BF16), VMEM((2, n_loc, 2 * cap, half), BF16), VMEM((8, n_loc, 2 * cap, half), BF16),
                 VMEM((16, tok, half), F32), VMEM((13, tok, half), F32), VMEM((8, tok, half), F32),
-                VMEM((tok, half), BF16), VMEM((tok, half), BF16),
+                VMEM((tok, half), BF16), VMEM((tok, half), BF16), VMEM((tok, half), BF16),
                 VMEM((2, 256, ffn), F32), VMEM((2, 256, ffn), F32),
                 DMA((5,)), DMA((3,)), DMA((2, 2)), DMA((2,)), DMA((2,)), DMA((2, 2)), DMA((1,)),
-                DMA((16, 4, 2)), DMA((16, 2)), DMA((16,)), DMA((16,)), DMA((8, n_loc)), DMA((8, n_loc)), DMA((8, 2)), DMA((8, 2)), DMA((10, 2)), DMA((13, 2)), DMA((2,)), DMA((2,)),
+                DMA((16, 4, 2)), DMA((16, 2)), DMA((16,)), DMA((16,)), DMA((8, n_loc)), DMA((8, n_loc)), DMA((8, 2)), DMA((8, 2)), DMA((10, 2)), DMA((13, 2)), DMA((2,)), DMA((2,)), DMA((2, 2)),
             ],
             compiler_params=pltpu.CompilerParams(collective_id=1, has_side_effects=True, vmem_limit_bytes=67043328),
             name="step",

time: 138 us -> 138 us (level)
  no operation moved by 1% of the time
where the time goes in v9:
time: 138 us; the launch traced here: 137 us
  Pallas kernels  136 us (99%)
    pallas_call x1, Pallas kernels, local_step(): pl.pallas_call(step_kernel, out_shape=(shape((tok, dim), BF16), shape((to...  127 us
    pallas_call x1, Pallas kernels, deliver(): pl.pallas_call(deliver_kernel, out_shape=tuple((jax.ShapeDtypeStruct(a.sh...  9.41 us

profile of v9, /device:TPU:19, one launch (start us, length us, event | category | flops | bytes accessed | tf_op | source)
XLA Modules:
  0.0 137.3 jit_solution(147409579572266689)
XLA Ops:
  0.6 127.0 %step.1 = (bf16[256,1024]{1,0:T(8,128)(2,1)}, f32[8,256]{1,0:T(8,128)}, f32[2,512,1024]{2,1,0:T(8,128)}, f32[2,1024,512]{2,1,0:T(8,128)}, f32[2,1024,512]{2,1,0:T(8,128)}) custom-call(bf16[256,1024]{1,0:T(8,128)(2,1)} %gy_hbm.1, s32[8,256]{1,0:T(8,128)} %bitcast.6, s32[8,256]{1,0:T(8,128)} %bitcast.7, f32[8,256]{1,0:T(8,128)} %bitcast.8, ...), custom_call_target="tpu_custom_call" | custom-call | tf_op jit(solution)/shard_map/step/pallas_call | solution.py:572
  127.7 9.4 %deliver.1 = (f32[2,1024,512]{2,1,0:T(8,128)}, f32[2,1024,512]{2,1,0:T(8,128)}, f32[2,512,1024]{2,1,0:T(8,128)}, bf16[256,1024]{1,0:T(8,128)(2,1)}, f32[8,256]{1,0:T(8,128)}) custom-call(f32[2,1024,512]{2,1,0:T(8,128)} %get-tuple-element.15.refs_0_, f32[2,1024,512]{2,1,0:T(8,128)} %get-tuple-element.16.refs_1_, f32[2,512,1024]{2,1,0:T(8,128)} %get-tuple-element.17.refs_2_, ...), custom_call_target="tpu_custom_call" | custom-call | tf_op jit(solution)/shard_map/deliver/pallas_call | solution.py:549
